TPU v7x, 256 devices: a whole 4x4x8 slice. The times are simulated.
256 devices in a mesh: batch: 8 (over x, core), cache: 32 (over y, z).
Axes of the slice: x: 4, y: 4, z: 8, core: 2. Of those that a mesh axis runs over, the one named last changes fastest.
Arguments:
- hidden_in: bfloat16 [64, 4096], P('batch'), may hold values from -6 to 6
- attn_gain: bfloat16 [4096], replicated, may hold values from 0.25 to 1.75
- w_query: bfloat16 [4096, 4096], P(None, 'cache'), may hold values from -0.09375 to 0.09375
- w_key: bfloat16 [4096, 1024], P(None, 'cache'), may hold values from -0.09375 to 0.09375
- w_value: bfloat16 [4096, 1024], P(None, 'cache'), may hold values from -0.09375 to 0.09375
- key_cache: bfloat16 [64, 4096, 1024], P('batch', 'cache'), may hold values from -400 to 400, as said below
- value_cache: bfloat16 [64, 4096, 1024], P('batch', 'cache'), may hold values from -6 to 6
- write_pos: int32 [64], P('batch'), may hold values from 0 to 12287, as said below
- cache_len: int32 [64], P('batch'), may hold values from 0 to 4095, as said below
- w_out: bfloat16 [4096, 4096], P('cache'), may hold values from -0.1875 to 0.1875
- mlp_gain: bfloat16 [4096], replicated, may hold values from 0.25 to 1.75
- w_gate: bfloat16 [4096, 7168], P(None, 'cache'), may hold values from -0.09375 to 0.09375
- w_up: bfloat16 [4096, 7168], P(None, 'cache'), may hold values from -0.09375 to 0.09375
- w_down: bfloat16 [7168, 4096], P('cache'), may hold values from -0.125 to 0.125
Outputs:
- hidden_out: bfloat16 [64, 4096], P('batch', 'cache')
Inputs may be any that keep to these rules, and one draw needn't show every extreme that they name: `key_cache`: keys of earlier tokens are finite reals. `write_pos`: positions of the new tokens; the largest value occurs in every draw. cache_len never exceeds write_pos; both 0 and 4095 occur in every draw, and many sequences attend fewer than 4095 earlier tokens.
All inputs are finite; a program needn't handle non-finite values.
Results may differ from a plain program's by a relative error of at most 0.017.
Values may be sent and summed in bfloat16 or wider, within the bound.
A program may use at most 64 MiB of HBM per device.

v0:
```python
import jax
import jax.numpy as jnp
from jax import lax
from jax.sharding import PartitionSpec as P

HEADS = 32
KV_HEADS = 8
HEAD_DIM = 128


def sent_together(arrays, axis, dim, along):
    widths = [a.shape[along] for a in arrays]
    both = jnp.concatenate(arrays, axis=along)
    out = lax.all_gather(both, axis, axis=dim, tiled=True)
    return tuple(jnp.split(out, [sum(widths[:k]) for k in range(1, len(widths))], axis=along))


def sent_to_all(x, axis):
    copies = jnp.broadcast_to(x, (lax.axis_size(axis), *x.shape))
    return lax.all_to_all(copies, axis, split_axis=0, concat_axis=0, tiled=True)


def of_everyone(x, axis):
    return sent_to_all(x, axis).max(axis=0)


def over_copies(x, axis):
    return sent_to_all(x, axis).sum(axis=0)


def cut_along(x, dim, devices):
    before, after = (x.shape[:dim], x.shape[dim + 1 :])
    return jnp.moveaxis(x.reshape(*before, devices, -1, *after), dim, 0)


def sum_at_owner(x, axis, dim):
    devices = lax.axis_size(axis)
    parts = lax.all_to_all(cut_along(x, dim, devices), axis, 0, 0, tiled=True)
    return jnp.sum(parts.astype(jnp.float32), axis=0)


def laid_out(parts, dim):
    parts = jnp.moveaxis(parts, 0, dim)
    lengths = parts.shape
    return parts.reshape(*lengths[:dim], lengths[dim] * lengths[dim + 1], *lengths[dim + 2 :])


def gather_directly(x, axis, dim):
    parts = sent_to_all(x, axis)
    return laid_out(parts, dim)


def rms_norm(values, gain):
    wide = values.astype(jnp.float32)
    spread = jnp.mean(wide * wide, axis=-1, keepdims=True)
    return (wide * lax.rsqrt(spread + 1e-05) * gain.astype(jnp.float32)).astype(jnp.bfloat16)


def rotate(heads, position):
    half = heads.shape[-1] // 2
    freq = 10000.0 ** (-(jnp.arange(half, dtype=jnp.float32) * 2.0 / heads.shape[-1]))
    angle = position.astype(jnp.float32)[:, None] * freq[None, :]
    cosine = jnp.cos(angle)[:, None, :]
    sine = jnp.sin(angle)[:, None, :]
    first = heads[..., :half]
    second = heads[..., half:]
    return jnp.concatenate(
        [first * cosine - second * sine, second * cosine + first * sine], axis=-1
    )


def per_device(
    hidden_in,
    attn_gain,
    w_query,
    w_key,
    w_value,
    key_cache,
    value_cache,
    write_pos,
    cache_len,
    w_out,
    mlp_gain,
    w_gate,
    w_up,
    w_down,
):
    seqs = hidden_in.shape[0]
    embedding_width = hidden_in.shape[1]
    ncache = lax.axis_size("cache")
    position_index = lax.axis_index("cache")
    slots_dev = key_cache.shape[1]
    window = slots_dev * ncache
    group = HEADS // KV_HEADS
    scale = 1.0 / HEAD_DIM**0.5
    feature_width = embedding_width // ncache
    normed = rms_norm(hidden_in, attn_gain)
    query_slice = jnp.dot(normed, w_query, preferred_element_type=jnp.float32).astype(jnp.bfloat16)
    key_part = jnp.dot(normed, w_key, preferred_element_type=jnp.float32).astype(jnp.bfloat16)
    value_part = jnp.dot(normed, w_value, preferred_element_type=jnp.float32).astype(jnp.bfloat16)
    query_raw, key_raw, value_new = (
        lax.all_gather(query_slice, "cache", axis=1, tiled=True),
        *sent_together((key_part, value_part), "cache", 1, 0),
    )
    query = rotate(query_raw.astype(jnp.float32).reshape(seqs, HEADS, HEAD_DIM), write_pos).astype(
        jnp.bfloat16
    )
    fresh_key_row = rotate(
        key_raw.astype(jnp.float32).reshape(seqs, KV_HEADS, HEAD_DIM), write_pos
    ).astype(jnp.bfloat16)
    value_heads = value_new.reshape(seqs, KV_HEADS, HEAD_DIM)
    slots = position_index * slots_dev + jnp.arange(slots_dev, dtype=jnp.int32)
    dist = (write_pos[:, None] - 1 - slots[None, :]) % window + 1
    valid = dist <= cache_len[:, None]
    owner = write_pos % window // slots_dev == position_index
    query_head_group = query.reshape(seqs, KV_HEADS, group, HEAD_DIM)
    keys = key_cache.reshape(seqs, slots_dev, KV_HEADS, HEAD_DIM)
    values = value_cache.reshape(seqs, slots_dev, KV_HEADS, HEAD_DIM)
    scores = (
        jnp.einsum("bkgd,bwkd->bkgw", query_head_group, keys, preferred_element_type=jnp.float32)
        * scale
    )
    own = (
        jnp.einsum(
            "vyjf,vyf->vyj", query_head_group, fresh_key_row, preferred_element_type=jnp.float32
        )
        * scale
    )
    scores = jnp.where(valid[:, None, None, :], scores, -1e30)
    own = jnp.where(owner[:, None, None], own, -1e30)
    top = jnp.maximum(jnp.max(scores, axis=-1), own)
    weights = jnp.where(valid[:, None, None, :], jnp.exp(scores - top[..., None]), 0.0)
    own_weight = jnp.where(owner[:, None, None], jnp.exp(own - top), 0.0)
    total = jnp.sum(weights, axis=-1) + own_weight
    own_low = lax.optimization_barrier(own_weight.astype(jnp.bfloat16)).astype(jnp.float32)
    reduced_total = jnp.einsum(
        "bkgw,bwkd->bkgd", weights.astype(jnp.bfloat16), values, preferred_element_type=jnp.float32
    )
    reduced_total = (
        reduced_total + own_low[..., None] * value_heads.astype(jnp.float32)[:, :, None, :]
    )
    top_flat = top.reshape(seqs, HEADS)
    total_flat = total.reshape(seqs, HEADS)
    summed_flat = reduced_total.reshape(seqs, HEADS, HEAD_DIM)
    largest = of_everyone(top_flat, "cache")
    factor = jnp.exp(top_flat - largest)
    scaled_total = over_copies(total_flat * factor, "cache")
    scaled_sum = (summed_flat * factor[..., None]).reshape(seqs, HEADS * HEAD_DIM)
    local_partial_sum = sum_at_owner(scaled_sum.astype(jnp.bfloat16), "cache", 1)
    total_features = jnp.repeat(scaled_total, HEAD_DIM, axis=1)
    own_total = lax.dynamic_slice_in_dim(
        total_features, position_index * feature_width, feature_width, 1
    )
    attended = (local_partial_sum / own_total).astype(jnp.bfloat16)
    projected = jnp.dot(attended, w_out, preferred_element_type=jnp.float32)
    share = sum_at_owner(projected.astype(jnp.bfloat16), "cache", 1)
    hidden_share = lax.dynamic_slice_in_dim(
        hidden_in, position_index * feature_width, feature_width, 1
    )
    mid_own = (hidden_share.astype(jnp.float32) + share).astype(jnp.bfloat16)
    mid_wide = mid_own.astype(jnp.float32)
    squares = over_copies(jnp.sum(mid_wide * mid_wide, axis=-1), "cache")
    gain_share = lax.dynamic_slice_in_dim(
        mlp_gain, position_index * feature_width, feature_width, 0
    )
    normed_share = (
        mid_wide
        * lax.rsqrt(squares / embedding_width + 1e-05)[:, None]
        * gain_share.astype(jnp.float32)
    ).astype(jnp.bfloat16)
    normed_mid = gather_directly(normed_share, "cache", 1)
    gate = jnp.dot(normed_mid, w_gate, preferred_element_type=jnp.float32)
    upper = jnp.dot(normed_mid, w_up, preferred_element_type=jnp.float32)
    act = (jax.nn.silu(gate) * upper).astype(jnp.bfloat16)
    down = jnp.dot(act, w_down, preferred_element_type=jnp.float32)
    down_own = sum_at_owner(down.astype(jnp.bfloat16), "cache", 1)
    return (mid_own.astype(jnp.float32) + down_own).astype(jnp.bfloat16)


def solution(mesh):
    in_specs = (
        P("batch", None),
        P(),
        P(None, "cache"),
        P(None, "cache"),
        P(None, "cache"),
        P("batch", "cache", None),
        P("batch", "cache", None),
        P("batch"),
        P("batch"),
        P("cache", None),
        P(),
        P(None, "cache"),
        P(None, "cache"),
        P("cache", None),
    )
    out_specs = P("batch", "cache")
    return jax.shard_map(
        per_device, mesh=mesh, in_specs=in_specs, out_specs=out_specs, check_vma=False
    )
```

profile of v0, /device:TPU:6, one launch (start us, length us, event | category | flops | bytes accessed | tf_op | source)
XLA Modules:
  0.0 211.6 jit_solution(16157100261924183315)
XLA Ops:
  0.0 0.8 fusion.62
  0.8 0.7 fusion.52
  1.5 1.0 fusion.18
  2.5 0.7 convert_element_type.92
  3.2 1.2 convolution_convert_fusion.3
  4.5 1.2 convolution_convert_fusion.2
  5.7 1.6 convolution_convert_fusion.4
  7.3 52.3 %all_gather.6 = bf16[8,4096]{1,0:T(8,128)(2,1)S(1)} all-gather(bf16[8,128]{1,0:T(8,128)(2,1)S(1)} %convolution_convert_fusion.4), channel_id=1, replica_groups=mesh['batch'=8,'cache'=32] {'cache'}, dimensions={1}, use_global_device_ids=true | all-gather | bytes 67584 | tf_op jit(solution)/shard_map/all_gather | solution.py:102
  59.9 42.2 %all-gather = bf16[32,32,16]{1,2,0:T(8,128)(2,1)S(1)} all-gather(bf16[1,32,16]{1,2,0:T(8,128)(2,1)S(1)} %maximum_bitcast_fusion.1), channel_id=1, replica_groups=mesh['batch'=8,'cache'=32] {'cache'}, dimensions={0}, use_global_device_ids=true | all-gather | bytes 33792 | tf_op jit(solution)/shard_map/all_gather | solution.py:14
  102.9 1.3 fusion.63
  104.5 0.7 reshape.212
  105.2 5.7 %all-to-all-start = ((f32[32,1,256]{2,1,0:T(1,128)}), f32[32,1,256]{2,1,0:T(1,128)S(1)}, u32[]{:S(2)}, u32[]{:S(2)}) async-start(f32[32,1,256]{2,1,0:T(1,128)} %reshape.212), calls=%async_computation | async-start | bytes 65536 | tf_op jit(solution)/shard_map/all_to_all | solution.py:20
  111.3 2.4 %fusion.12 = f32[8,8,4,128]{3,2,1,0:T(4,128)S(1)} fusion(f32[8,8,4,128]{3,2,1,0:T(4,128)S(1)} %get-tuple-element.22, f32[8,8,128]{2,1,0:T(8,128)S(1)} %copy.60, f32[8,8,4]{2,1,0:T(8,128)S(1)} %convert_element_type.100, f32[8,8,4]{2,1,0:T(8,128)S(1)} %fusion.35, pred[8,128]{1,0:T(8,128)(4,1)S(1)} %fusion.44, bf16[8,128,1024]{2,1,0:T(8,128)(2,1)} %param.20), kind=kOutput, calls=%fused_computation.10 | convolution fusion | flops 8552448 | bytes 2395136 | tf_op jit(solution)/shard_map/bkgw,bwkd->bkgd/dot_general | solution.py:136
  113.9 6.9 %all-to-all-done = f32[32,1,256]{2,1,0:T(1,128)S(1)} async-done(((f32[32,1,256]{2,1,0:T(1,128)}), f32[32,1,256]{2,1,0:T(1,128)S(1)}, u32[]{:S(2)}, u32[]{:S(2)}) %all-to-all-start) | async-done | bytes 32800 | tf_op jit(solution)/shard_map/all_to_all | solution.py:20
  121.3 0.7 reduce.1
  122.3 0.7 reshape.214
  123.0 3.8 %all-to-all-start.2 = ((f32[32,1,256]{2,1,0:T(1,128)}), f32[32,1,256]{2,1,0:T(1,128)S(1)}, u32[]{:S(2)}, u32[]{:S(2)}) async-start(f32[32,1,256]{2,1,0:T(1,128)} %reshape.214), calls=%async_computation.2 | async-start | bytes 65536 | tf_op jit(solution)/shard_map/all_to_all | solution.py:20
  126.8 0.7 fusion.25
  127.6 9.1 %all-to-all-done.2 = f32[32,1,256]{2,1,0:T(1,128)S(1)} async-done(((f32[32,1,256]{2,1,0:T(1,128)}), f32[32,1,256]{2,1,0:T(1,128)S(1)}, u32[]{:S(2)}, u32[]{:S(2)}) %all-to-all-start.2) | async-done | bytes 32800 | tf_op jit(solution)/shard_map/all_to_all | solution.py:20
  136.7 3.9 %all-to-all-start.1 = ((bf16[32,8,128]{2,1,0:T(8,128)(2,1)}), bf16[32,8,128]{2,1,0:T(8,128)(2,1)S(1)}, u32[]{:S(2)}, u32[]{:S(2)}) async-start(bf16[32,8,128]{2,1,0:T(8,128)(2,1)} %fusion.25), calls=%async_computation.1 | async-start | bytes 131072 | tf_op jit(solution)/shard_map/all_to_all | solution.py:38
  140.6 0.7 reduce.2
  141.6 9.0 %all-to-all-done.1 = bf16[32,8,128]{2,1,0:T(8,128)(2,1)S(1)} async-done(((bf16[32,8,128]{2,1,0:T(8,128)(2,1)}), bf16[32,8,128]{2,1,0:T(8,128)(2,1)S(1)}, u32[]{:S(2)}, u32[]{:S(2)}) %all-to-all-start.1) | async-done | bytes 65568 | tf_op jit(solution)/shard_map/all_to_all | solution.py:38
  150.9 13.2 %all_to_all.36 = bf16[32,8,128]{2,1,0:T(8,128)(2,1)S(1)} all-to-all(bf16[32,8,128]{2,1,0:T(8,128)(2,1)S(1)} %fusion.15), channel_id=1, replica_groups=mesh['batch'=8,'cache'=32] {'cache'}, dimensions={0} | all-to-all | bytes 131072 | tf_op jit(solution)/shard_map/all_to_all | solution.py:38
  164.1 0.8 fusion.45
  164.9 0.6 broadcast_in_dim.83
  165.5 3.9 %all-to-all-start.4 = ((f32[32,1,8]{2,1,0:T(1,128)}), f32[32,1,8]{2,1,0:T(1,128)S(1)}, u32[]{:S(2)}, u32[]{:S(2)}) async-start(f32[32,1,8]{2,1,0:T(1,128)} %broadcast_in_dim.83), calls=%async_computation.4 | async-start | bytes 32768 | tf_op jit(solution)/shard_map/all_to_all | solution.py:20
  169.3 0.8 dynamic-slice_convert_fusion
  170.1 9.1 %all-to-all-done.4 = f32[32,1,8]{2,1,0:T(1,128)S(1)} async-done(((f32[32,1,8]{2,1,0:T(1,128)}), f32[32,1,8]{2,1,0:T(1,128)S(1)}, u32[]{:S(2)}, u32[]{:S(2)}) %all-to-all-start.4) | async-done | bytes 1056 | tf_op jit(solution)/shard_map/all_to_all | solution.py:20
  179.3 13.0 %all_to_all.37 = bf16[32,8,128]{2,1,0:T(8,128)(2,1)S(1)} all-to-all(bf16[32,8,128]{2,1,0:T(8,128)(2,1)S(1)} %broadcast_in_dim.84), channel_id=1, replica_groups=mesh['batch'=8,'cache'=32] {'cache'}, dimensions={0} | all-to-all | bytes 131072 | tf_op jit(solution)/shard_map/all_to_all | solution.py:20
  192.3 2.1 fusion.28
  194.3 3.4 %fusion.16 = bf16[32,8,128]{2,1,0:T(8,128)(2,1)S(1)} fusion(bf16[224,4096]{1,0:T(8,128)(2,1)} %param.27, bf16[4096,224]{0,1:T(8,128)(2,1)} %param.26, bf16[32,8,128]{2,1,0:T(8,128)(2,1)S(1)} %all_to_all.37, f32[8,224]{1,0:T(8,128)S(1)} %fusion.28), kind=kOutput, calls=%fused_computation.12 | convolution fusion | flops 29403648 | bytes 3808256 | tf_op jit(solution)/shard_map/dot_general | solution.py:175
  197.8 13.2 %all_to_all.38 = bf16[32,8,128]{2,1,0:T(8,128)(2,1)S(1)} all-to-all(bf16[32,8,128]{2,1,0:T(8,128)(2,1)S(1)} %fusion.16), channel_id=1, replica_groups=mesh['batch'=8,'cache'=32] {'cache'}, dimensions={0} | all-to-all | bytes 131072 | tf_op jit(solution)/shard_map/all_to_all | solution.py:38
  (51 shorter events, 4.0 us)
Async XLA Ops:
  0.0 102.9 %copy-start = (bf16[8,128,1024]{2,1,0:T(8,128)(2,1)S(1)}, bf16[8,128,1024]{2,1,0:T(8,128)(2,1)}, u32[]{:S(2)}) copy-start(bf16[8,128,1024]{2,1,0:T(8,128)(2,1)} %param.19) | copy-start | bytes 6291460
  0.0 102.5 %copy-start.2 = (s32[8]{0:T(128)S(1)}, s32[8]{0:T(128)}, u32[]{:S(2)}) copy-start(s32[8]{0:T(128)} %param.22) | copy-start | bytes 100
  105.2 15.6 %all-to-all-start = ((f32[32,1,256]{2,1,0:T(1,128)}), f32[32,1,256]{2,1,0:T(1,128)S(1)}, u32[]{:S(2)}, u32[]{:S(2)}) async-start(f32[32,1,256]{2,1,0:T(1,128)} %reshape.212), calls=%async_computation | async-start | bytes 65536 | tf_op jit(solution)/shard_map/all_to_all | solution.py:20
  111.3 39.3 %copy-start.1 = (bf16[128,4096]{1,0:T(8,128)(2,1)S(1)}, bf16[128,4096]{1,0:T(8,128)(2,1)}, u32[]{:S(2)}) copy-start(bf16[128,4096]{1,0:T(8,128)(2,1)} %param.23) | copy-start | bytes 3145732
  123.0 13.7 %all-to-all-start.2 = ((f32[32,1,256]{2,1,0:T(1,128)}), f32[32,1,256]{2,1,0:T(1,128)S(1)}, u32[]{:S(2)}, u32[]{:S(2)}) async-start(f32[32,1,256]{2,1,0:T(1,128)} %reshape.214), calls=%async_computation.2 | async-start | bytes 65536 | tf_op jit(solution)/shard_map/all_to_all | solution.py:20
  136.7 13.9 %all-to-all-start.1 = ((bf16[32,8,128]{2,1,0:T(8,128)(2,1)}), bf16[32,8,128]{2,1,0:T(8,128)(2,1)S(1)}, u32[]{:S(2)}, u32[]{:S(2)}) async-start(bf16[32,8,128]{2,1,0:T(8,128)(2,1)} %fusion.25), calls=%async_computation.1 | async-start | bytes 131072 | tf_op jit(solution)/shard_map/all_to_all | solution.py:38
  165.5 13.7 %all-to-all-start.4 = ((f32[32,1,8]{2,1,0:T(1,128)}), f32[32,1,8]{2,1,0:T(1,128)S(1)}, u32[]{:S(2)}, u32[]{:S(2)}) async-start(f32[32,1,8]{2,1,0:T(1,128)} %broadcast_in_dim.83), calls=%async_computation.4 | async-start | bytes 32768 | tf_op jit(solution)/shard_map/all_to_all | solution.py:20
where the time goes:
time: 212 us
  blocking collectives  134 us (63%)
  waiting for transfers between devices  34.1 us (16%)
  starting transfers between devices  17.2 us (8%)
  matrix products  13.7 us (6%)
  other arithmetic  8.78 us (4%)
  local copies, waits for them, and re-layouts  3.68 us (2%)
    all_gather x1, blocking collectives, per_device(): lax.all_gather(query_slice, 'cache', axis=1, tiled=True)  52.3 us
    all_gather x1, blocking collectives, sent_together(): out = lax.all_gather(both, axis, axis=dim, tiled=True)  42.2 us
    all_to_all x2, blocking collectives, sum_at_owner(): parts = lax.all_to_all(cut_along(x, dim, devices), axis, 0, 0, tiled=True)  26.3 us
    all_to_all x3, waiting for transfers between devices, sent_to_all(): return lax.all_to_all(copies, axis, split_axis=0, concat_axis=0, tiled=True)  25.1 us
    all_to_all x3, starting transfers between devices, sent_to_all(): return lax.all_to_all(copies, axis, split_axis=0, concat_axis=0, tiled=True)  13.3 us
    all_to_all x1, blocking collectives, sent_to_all(): return lax.all_to_all(copies, axis, split_axis=0, concat_axis=0, tiled=True)  13 us
    all_to_all x1, waiting for transfers between devices, sum_at_owner(): parts = lax.all_to_all(cut_along(x, dim, devices), axis, 0, 0, tiled=True)  8.97 us
  transfers between devices with their start and end apart: 4, of which 4 were waited for; matrix products, arithmetic and copies ran while one was open for 3% of the time, Pallas kernels for 0%

commit v1 on v0

v1 whole, which is shorter than its diff:
```python
import functools
import math

import jax
import jax.numpy as jnp
from jax import lax
from jax.experimental import pallas as pl
from jax.experimental.pallas import tpu as pltpu
from jax.sharding import PartitionSpec as P

HEADS = 32
KV_HEADS = 8
HEAD_DIM = 128
GROUP = HEADS // KV_HEADS
NY, NZ = 4, 8
N = NY * NZ
LOW = -1e30
MESH = pl.DeviceIdType.MESH
F32 = jnp.float32
BF16 = jnp.bfloat16

OFFSETS = sorted(
    [(dy, dz) for dy in range(NY) for dz in range(NZ) if (dy, dz) != (0, 0)],
    key=lambda t: -(min(t[0], NY - t[0]) + min(t[1], NZ - t[1])),
)


def row_sum(x):
    return jnp.sum(x, axis=-1, keepdims=True)


def dot_rows(a, b):
    return lax.dot_general(a, b, (((1,), (1,)), ((), ())), preferred_element_type=F32)


def split3(x):
    high = x.astype(BF16)
    rest = x - high.astype(F32)
    mid = rest.astype(BF16)
    low = (rest - mid.astype(F32)).astype(BF16)
    return high, mid, low


def kernel(
    hidden_hbm, gain_hbm, wq_hbm, wk_hbm, wv_hbm, kc_hbm, vc_hbm, pos_ref, len_ref,
    wo_hbm, mgain_hbm, wg_hbm, wu_hbm, wd_hbm,
    out_ref,
    hidden, gain, wq, wk, wv, kc, vc, wo, mgain, wg, wu, wd,
    qbuf, kvbuf, osend, orecv, psend, precv, midbuf, dsend, drecv,
    load_sem, send_sem, recv_sem, kv_send, kv_recv,
):
    me = lax.axis_index("cache")
    y, z = me // NZ, lax.rem(me, NZ)
    seqs = hidden.shape[0]
    width = hidden.shape[1]
    slots = kc.shape[1]

    peers = []
    for dy, dz in OFFSETS:
        peers.append((dy * NZ + dz, lax.rem(y + dy, NY) * NZ + lax.rem(z + dz, NZ)))

    def source(offset):
        dy, dz = offset // NZ, offset % NZ
        return lax.rem(y + NY - dy, NY) * NZ + lax.rem(z + NZ - dz, NZ)

    barrier = pltpu.get_barrier_semaphore()
    for _, peer in peers:
        pl.semaphore_signal(barrier, inc=1, device_id={"cache": peer}, device_id_type=MESH)

    pairs = [
        (hidden_hbm, hidden), (gain_hbm, gain), (wq_hbm, wq), (wk_hbm, wk), (wv_hbm, wv), (kc_hbm, kc),
        (vc_hbm, vc), (wo_hbm, wo), (mgain_hbm, mgain), (wg_hbm, wg), (wu_hbm, wu), (wd_hbm, wd),
    ]
    loads = [pltpu.make_async_copy(a, b, load_sem.at[i]) for i, (a, b) in enumerate(pairs)]
    for copy in loads:
        copy.start()
    l_hidden, l_gain, l_wq, l_wk, l_wv, l_kc, l_vc, l_wo, l_mgain, l_wg, l_wu, l_wd = loads

    def send_all(phase, piece, dst):
        copies = []
        for offset, peer in peers:
            copy = pltpu.make_async_remote_copy(
                src_ref=piece(peer), dst_ref=dst(offset), send_sem=send_sem.at[phase, offset],
                recv_sem=recv_sem.at[phase, offset], device_id={"cache": peer}, device_id_type=MESH,
            )
            copy.start()
            copies.append(copy)
        return copies

    lane = lax.broadcasted_iota(jnp.int32, (seqs, HEAD_DIM), 1)
    row = lax.broadcasted_iota(jnp.int32, (seqs, HEAD_DIM), 0)
    half = HEAD_DIM // 2
    pos = jnp.zeros((seqs, HEAD_DIM), jnp.int32)
    length = jnp.zeros((seqs, HEAD_DIM), jnp.int32)
    for s in range(seqs):
        pos = jnp.where(row == s, pos_ref[s], pos)
        length = jnp.where(row == s, len_ref[s], length)
    freq = jnp.exp(lax.rem(lane, half).astype(F32) * (-math.log(10000.0) / half))
    angle = pos.astype(F32) * freq
    cosine = jnp.cos(angle)
    sine = jnp.sin(angle) * jnp.where(lane < half, -1.0, 1.0)

    def rotate(x):
        return x * cosine + pltpu.roll(x, half, 1) * sine

    slot = me * slots + lane
    dist = jnp.bitwise_and(pos - 1 - slot, slots * N - 1) + 1
    valid = dist <= length

    l_hidden.wait()
    l_gain.wait()
    wide = hidden[...].astype(F32)
    scale = lax.rsqrt(row_sum(wide * wide) / width + 1e-5)
    chunks = []
    for c in range(width // 128):
        part = wide[:, c * 128 : (c + 1) * 128] * scale * gain[c : c + 1, :].astype(F32)
        chunks.append(part.astype(BF16))
    normed = jnp.concatenate(chunks, axis=1)
    l_wq.wait()
    query = jnp.dot(normed, wq[...], preferred_element_type=F32).astype(BF16).astype(F32)
    query = rotate(query).astype(BF16)
    qbuf[me] = query
    l_wk.wait()
    l_wv.wait()
    key_part = dot_rows(normed, wk[...]).astype(BF16)
    value_part = dot_rows(normed, wv[...]).astype(BF16)
    quarter = HEAD_DIM // GROUP
    place = lax.broadcasted_iota(jnp.int32, (quarter, HEAD_DIM), 1)
    origin = lax.broadcasted_iota(jnp.int32, (quarter, HEAD_DIM), 0)
    member = lax.rem(me, GROUP)
    spread = jnp.where(place == origin + member * quarter, 1.0, 0.0).astype(BF16)
    kvbuf[0, 0] = jnp.dot(key_part, spread, preferred_element_type=F32).astype(BF16)
    kvbuf[0, 1] = jnp.dot(value_part, spread, preferred_element_type=F32).astype(BF16)

    pl.semaphore_wait(barrier, N - 1)

    q_copies = send_all(0, lambda p: qbuf.at[me], lambda k: qbuf.at[me])
    kv_copies = []
    for k in range(1, GROUP):
        peer = me - member + lax.rem(member + k, GROUP)
        copy = pltpu.make_async_remote_copy(
            src_ref=kvbuf.at[0], dst_ref=kvbuf.at[k], send_sem=kv_send.at[k], recv_sem=kv_recv.at[k],
            device_id={"cache": peer}, device_id_type=MESH,
        )
        copy.start()
        kv_copies.append(copy)

    l_kc.wait()
    l_vc.wait()
    for copy in q_copies:
        copy.wait_recv()

    rows = GROUP * seqs
    row4 = lax.broadcasted_iota(jnp.int32, (rows, HEAD_DIM), 0)
    pick = [jnp.where(lax.rem(row4, seqs) == s, 1.0, 0.0).astype(BF16) for s in range(seqs)]
    valid4 = jnp.concatenate([valid] * GROUP, axis=0)
    lane4 = lax.rem(lax.broadcasted_iota(jnp.int32, (rows, HEAD_DIM), 1), 4)
    for g in range(KV_HEADS):
        cols = pl.ds(g * HEAD_DIM, HEAD_DIM)
        qg = qbuf[pl.ds(g * GROUP, GROUP)].reshape(rows, HEAD_DIM)
        left = jnp.concatenate([qg * pick[s] for s in range(seqs)], axis=1)
        keys = jnp.concatenate([kc[s, :, cols] for s in range(seqs)], axis=1)
        scores = dot_rows(left, keys)
        scores = jnp.where(valid4, scores * (1.0 / math.sqrt(HEAD_DIM)), LOW)
        top = jnp.max(scores, axis=-1, keepdims=True)
        weights = jnp.where(valid4, jnp.exp(scores - top), 0.0)
        total = row_sum(weights)
        low = weights.astype(BF16)
        left = jnp.concatenate([low * pick[s] for s in range(seqs)], axis=1)
        values = jnp.concatenate([vc[s, :, cols] for s in range(seqs)], axis=0)
        summed = jnp.dot(left, values, preferred_element_type=F32)
        some = total > 0.0
        safe = jnp.where(some, total, 1.0)
        share = (summed * (1.0 / safe)).astype(BF16)
        level = jnp.broadcast_to(jnp.where(some, top + jnp.log(safe), LOW), (rows, HEAD_DIM))
        high, mid, low3 = split3(level)
        stat = jnp.where(
            lane4 == 0, high.astype(F32), jnp.where(lane4 == 1, mid.astype(F32), jnp.where(lane4 == 2, low3.astype(F32), 0.0))
        ).astype(BF16)
        osend[pl.ds(g * GROUP, GROUP), 0] = share.reshape(GROUP, seqs, HEAD_DIM)
        osend[pl.ds(g * GROUP, GROUP), 1] = stat.reshape(GROUP, seqs, HEAD_DIM)

    o_copies = send_all(1, lambda p: osend.at[p], lambda k: orecv.at[k])

    for copy in kv_copies:
        copy.wait_recv()
    key_raw = kvbuf[0, 0].astype(F32)
    value_new = kvbuf[0, 1].astype(F32)
    for k in range(1, GROUP):
        key_raw = key_raw + kvbuf[k, 0].astype(F32)
        value_new = value_new + kvbuf[k, 1].astype(F32)
    key_new = rotate(key_raw).astype(BF16).astype(F32)
    own = row_sum(qbuf[me].astype(F32) * key_new) * (1.0 / math.sqrt(HEAD_DIM))
    own = jnp.broadcast_to(own, (seqs, HEAD_DIM))

    def level_of(stat):
        pair = stat + pltpu.roll(stat, 1, 1)
        return pair + pltpu.roll(pair, 2, 1)

    for copy in o_copies:
        copy.wait_recv()
    levels = [level_of(osend[me, 1].astype(F32))]
    for k in range(1, N):
        levels.append(level_of(orecv[k, 1].astype(F32)))
    peak = own
    for level in levels:
        peak = jnp.maximum(peak, level)
    factor = jnp.exp(own - peak)
    weight_sum = factor
    number = factor * value_new
    for k in range(N):
        share = (osend[me, 0] if k == 0 else orecv[k, 0]).astype(F32)
        factor = jnp.exp(levels[k] - peak)
        weight_sum = weight_sum + factor
        number = number + factor * share
    attended = (number / weight_sum).astype(BF16)

    def scatter(phase, left, weight, stage, landing):
        for c in range(N):
            part = jnp.dot(left, weight[:, c * 128 : (c + 1) * 128], preferred_element_type=F32)
            stage[c] = part.astype(BF16)
        return send_all(phase, lambda p: stage.at[p], lambda k: landing.at[k])

    def gathered(copies, stage, landing):
        for copy in copies:
            copy.wait_recv()
        total = stage[me].astype(F32)
        for k in range(1, N):
            total = total + landing[k].astype(F32)
        return total

    l_wo.wait()
    p_copies = scatter(2, attended, wo, psend, precv)
    mine = pl.ds(pl.multiple_of(me * 128, 128), 128)
    mid_own = (hidden[:, mine].astype(F32) + gathered(p_copies, psend, precv)).astype(BF16)
    midbuf[me] = mid_own
    m_copies = send_all(3, lambda p: midbuf.at[me], lambda k: midbuf.at[me])
    l_mgain.wait()
    l_wg.wait()
    l_wu.wait()
    l_wd.wait()
    for copy in m_copies:
        copy.wait_recv()
    squares = jnp.zeros((seqs, 128), F32)
    for c in range(N):
        part = midbuf[c].astype(F32)
        squares = squares + part * part
    scale = lax.rsqrt(row_sum(squares) / width + 1e-5)
    chunks = []
    for c in range(N):
        chunks.append((midbuf[c].astype(F32) * scale * mgain[c : c + 1, :].astype(F32)).astype(BF16))
    normed_mid = jnp.concatenate(chunks, axis=1)
    gate = dot_rows(normed_mid, wg[...])
    upper = dot_rows(normed_mid, wu[...])
    act = (gate / (1.0 + jnp.exp(-gate)) * upper).astype(BF16)
    d_copies = scatter(4, act, wd, dsend, drecv)
    total = gathered(d_copies, dsend, drecv)
    out_ref[...] = (mid_own.astype(F32) + total).astype(BF16)

    for copy in q_copies + kv_copies + o_copies + p_copies + m_copies + d_copies:
        copy.wait_send()


def per_device(*args):
    (hidden_in, attn_gain, w_query, w_key, w_value, key_cache, value_cache, write_pos, cache_len, w_out, mlp_gain,
     w_gate, w_up, w_down) = args
    seqs, width = hidden_in.shape
    lines = width // 128
    attn_gain = attn_gain.reshape(lines, 128)
    mlp_gain = mlp_gain.reshape(lines, 128)
    w_key, w_value, w_gate, w_up = w_key.T, w_value.T, w_gate.T, w_up.T
    any_space = pl.BlockSpec(memory_space=pl.ANY)
    smem = pl.BlockSpec(memory_space=pltpu.SMEM)
    operands = (hidden_in, attn_gain, w_query, w_key, w_value, key_cache, value_cache, write_pos, cache_len, w_out,
                mlp_gain, w_gate, w_up, w_down)
    loaded = [a for a in operands if a is not write_pos and a is not cache_len]
    block = (N, seqs, 128)
    return pl.pallas_call(
        kernel,
        out_shape=jax.ShapeDtypeStruct((seqs, 128), BF16),
        in_specs=[any_space] * 7 + [smem] * 2 + [any_space] * 5,
        out_specs=pl.BlockSpec(memory_space=pltpu.VMEM),
        scratch_shapes=[pltpu.VMEM(a.shape, a.dtype) for a in loaded]
        + [
            pltpu.VMEM(block, BF16),
            pltpu.VMEM((GROUP, 2, seqs, 128), BF16),
            pltpu.VMEM((N, 2, seqs, 128), BF16),
            pltpu.VMEM((N, 2, seqs, 128), BF16),
            pltpu.VMEM(block, BF16),
            pltpu.VMEM(block, BF16),
            pltpu.VMEM(block, BF16),
            pltpu.VMEM(block, BF16),
            pltpu.VMEM(block, BF16),
            pltpu.SemaphoreType.DMA((len(loaded),)),
            pltpu.SemaphoreType.DMA((5, N)),
            pltpu.SemaphoreType.DMA((5, N)),
            pltpu.SemaphoreType.DMA((GROUP,)),
            pltpu.SemaphoreType.DMA((GROUP,)),
        ],
        compiler_params=pltpu.CompilerParams(
            collective_id=0, has_side_effects=True, vmem_limit_bytes=60 * 1024 * 1024
        ),
    )(*operands)


def solution(mesh):
    in_specs = (
        P("batch", None),
        P(),
        P(None, "cache"),
        P(None, "cache"),
        P(None, "cache"),
        P("batch", "cache", None),
        P("batch", "cache", None),
        P("batch"),
        P("batch"),
        P("cache", None),
        P(),
        P(None, "cache"),
        P(None, "cache"),
        P("cache", None),
    )
    return jax.shard_map(
        per_device, mesh=mesh, in_specs=in_specs, out_specs=P("batch", "cache"), check_vma=False
    )
```

time: 212 us -> 49.7 us (0.23)
  blocking collectives: 134 us -> 0 us
  Pallas kernels: 0 us -> 48.4 us
  waiting for transfers between devices: 34.1 us -> 0 us
  starting transfers between devices: 17.2 us -> 0 us
  matrix products: 13.7 us -> 0 us
  other arithmetic: 8.78 us -> 0 us
  local copies, waits for them, and re-layouts: 3.68 us -> 1.26 us
    all_gather x2 -> x0, blocking collectives: 94.6 us -> none  [the longest x1 52.3 us: per_device(): lax.all_gather(query_slice, 'cache', axis=1, tiled=True)]
    pallas_call x0 -> x1, Pallas kernels: none -> 48.4 us  [per_device(): pl.pallas_call(kernel, out_shape=jax.ShapeDtypeStruct((seqs, 128), BF16),...]
    all_to_all x3 -> x0, blocking collectives: 39.3 us -> none  [the longest x2 26.3 us: sum_at_owner(): parts = lax.all_to_all(cut_along(x, dim, devices), axis, 0, 0, tiled=True)]
    all_to_all x4 -> x0, waiting for transfers between devices: 34.1 us -> none  [the longest x3 25.1 us: sent_to_all(): return lax.all_to_all(copies, axis, split_axis=0, concat_axis=0, tiled=True)]
    all_to_all x4 -> x0, starting transfers between devices: 17.2 us -> none  [the longest x3 13.3 us: sent_to_all(): return lax.all_to_all(copies, axis, split_axis=0, concat_axis=0, tiled=True)]
    dot_general x9 -> x0, matrix products: 13.7 us -> none  [the longest x1 3.44 us: per_device(): down = jnp.dot(act, w_down, preferred_element_type=jnp.float32)]
    convert_element_type x6 -> x0, other arithmetic: 2.96 us -> none  [the longest x1 0.83 us: rotate(): angle = position.astype(jnp.float32)[:, None] * freq[None, :]]
    reduce_sum x8 -> x0, other arithmetic: 2.25 us -> none  [the longest x1 0.99 us: rms_norm(): spread = jnp.mean(wide * wide, axis=-1, keepdims=True)]
  transfers between devices with their start and end apart: 4 -> 0, of which waited for: 4 -> 0; matrix products, arithmetic and copies ran while one was open for 3% -> 0% of each run, Pallas kernels for 0% -> 0%
where the time goes in v1:
time: 49.7 us; the launch traced here: 49.6 us
  Pallas kernels  48.4 us (97%)
  local copies, waits for them, and re-layouts  1.26 us (3%)
    pallas_call x1, Pallas kernels, per_device(): pl.pallas_call(kernel, out_shape=jax.ShapeDtypeStruct((seqs, 128), BF16),...  48.4 us
    unnamed x1, local copies, waits for them, and re-layouts  1.26 us

profile of v1, /device:TPU:6, one launch (start us, length us, event | category | flops | bytes accessed | tf_op | source)
XLA Modules:
  0.0 49.6 jit_solution(2673816923071842363)
XLA Ops:
  0.0 48.4 %shard_map.136 = bf16[8,128]{1,0:T(8,128)(2,1)} custom-call(bf16[8,4096]{1,0:T(8,128)(2,1)} %hidden_hbm.1, bf16[32,128]{1,0:T(8,128)(2,1)} %bitcast.10, bf16[4096,128]{1,0:T(8,128)(2,1)} %wq_hbm.1, bf16[32,4096]{1,0:T(8,128)(2,1)} %bitcast.8, bf16[32,4096]{1,0:T(8,128)(2,1)} %bitcast.9, bf16[8,128,1024]{2,1,0:T(8,128)(2,1)} %kc_hbm.1, ...), custom_call_target="tpu_custom_call" | custom-call | tf_op jit(solution)/shard_map/pallas_call | solution.py:278
  48.4 1.3 %copy.16 = bf16[8,128]{1,0:T(8,128)(2,1)} copy(bf16[8,128]{1,0:T(8,128)(2,1)} %shard_map.136) | data formatting | bytes 4096

commit v2 on v1

v2 whole, which is shorter than its diff:
```python
import functools
import math

import jax
import jax.numpy as jnp
from jax import lax
from jax.experimental import pallas as pl
from jax.experimental.pallas import tpu as pltpu
from jax.sharding import PartitionSpec as P

HEADS = 32
KV_HEADS = 8
HEAD_DIM = 128
GROUP = HEADS // KV_HEADS
NY, NZ = 4, 8
N = NY * NZ
LOW = -1e30
MESH = pl.DeviceIdType.MESH
F32 = jnp.float32
BF16 = jnp.bfloat16

OFFSETS = sorted(
    [(dy, dz) for dy in range(NY) for dz in range(NZ) if (dy, dz) != (0, 0)],
    key=lambda t: -(min(t[0], NY - t[0]) + min(t[1], NZ - t[1])),
)
DISTANCE = [min(dy, NY - dy) + min(dz, NZ - dz) for dy, dz in OFFSETS]
BATCHES = (((0, 0), (0, 1), (1, 0), (3, 0)), ((1, 1), (3, 1), (2, 0)), ((2, 1),))


def row_sum(x):
    return jnp.sum(x, axis=-1, keepdims=True)


def dot_rows(a, b):
    return lax.dot_general(a, b, (((1,), (1,)), ((), ())), preferred_element_type=F32)


def split3(x):
    high = x.astype(BF16)
    rest = x - high.astype(F32)
    mid = rest.astype(BF16)
    low = (rest - mid.astype(F32)).astype(BF16)
    return high, mid, low


def kernel(
    hidden_hbm, gain_hbm, wq_hbm, wk_hbm, wv_hbm, kc_hbm, vc_hbm, pos_hbm, len_hbm,
    wo_hbm, mgain_hbm, wg_hbm, wu_hbm, wd_hbm,
    out_ref,
    hidden, gain, wq, wk, wv, kc, vc, pos_ref, len_ref, wo, mgain, wg, wu, wd,
    qbuf, kvbuf, osend, orecv, psend, precv, midbuf, dsend, drecv, mgain_wide,
    load_sem, send_sem, recv_sem, kv_send, kv_recv,
):
    me = lax.axis_index("cache")
    y, z = me // NZ, lax.rem(me, NZ)
    seqs = hidden.shape[0]
    width = hidden.shape[1]
    slots = kc.shape[1]

    peers = [lax.rem(y + dy, NY) * NZ + lax.rem(z + dz, NZ) for dy, dz in OFFSETS]

    barrier = pltpu.get_barrier_semaphore()
    for peer in peers:
        pl.semaphore_signal(barrier, inc=1, device_id={"cache": peer}, device_id_type=MESH)

    pairs = [
        (hidden_hbm, hidden), (gain_hbm, gain), (pos_hbm, pos_ref), (len_hbm, len_ref), (wq_hbm, wq), (wk_hbm, wk),
        (wv_hbm, wv), (kc_hbm, kc), (vc_hbm, vc), (wo_hbm, wo), (mgain_hbm, mgain), (wg_hbm, wg), (wu_hbm, wu),
        (wd_hbm, wd),
    ]
    loads = [pltpu.make_async_copy(a, b, load_sem.at[i]) for i, (a, b) in enumerate(pairs)]
    for copy in loads:
        copy.start()
    l_hidden, l_gain, l_pos, l_len, l_wq, l_wk, l_wv, l_kc, l_vc, l_wo, l_mgain, l_wg, l_wu, l_wd = loads

    def send(phase, src, dst, peer):
        copy = pltpu.make_async_remote_copy(
            src_ref=src, dst_ref=dst, send_sem=send_sem.at[phase, peer], recv_sem=recv_sem.at[phase, me],
            device_id={"cache": peer}, device_id_type=MESH,
        )
        copy.start()
        return copy

    def arrived(phase, ref, peer):
        pltpu.make_async_remote_copy(
            src_ref=ref, dst_ref=ref, send_sem=send_sem.at[phase, peer], recv_sem=recv_sem.at[phase, peer],
            device_id={"cache": peer}, device_id_type=MESH,
        ).wait_recv()

    def sent(copies):
        for copy in copies:
            copy.wait_send()

    lane = lax.broadcasted_iota(jnp.int32, (seqs, HEAD_DIM), 1)
    row = lax.broadcasted_iota(jnp.int32, (seqs, HEAD_DIM), 0)
    half = HEAD_DIM // 2
    l_pos.wait()
    l_len.wait()
    pos = jnp.zeros((seqs, HEAD_DIM), jnp.int32)
    length = jnp.zeros((seqs, HEAD_DIM), jnp.int32)
    for s in range(seqs):
        pos = jnp.where(row == s, pos_ref[s], pos)
        length = jnp.where(row == s, len_ref[s], length)
    freq = jnp.exp(lax.rem(lane, half).astype(F32) * (-math.log(10000.0) / half))
    angle = pos.astype(F32) * freq
    cosine = jnp.cos(angle)
    sine = jnp.sin(angle) * jnp.where(lane < half, -1.0, 1.0)

    def rotate(x):
        return x * cosine + pltpu.roll(x, half, 1) * sine

    slot = me * slots + lane
    dist = jnp.bitwise_and(pos - 1 - slot, slots * N - 1) + 1
    valid = dist <= length

    l_hidden.wait()
    l_gain.wait()
    wide = hidden[...].astype(F32)
    scale = lax.rsqrt(row_sum(wide * wide) / width + 1e-5)
    chunks = []
    for c in range(width // 128):
        part = wide[:, c * 128 : (c + 1) * 128] * scale * gain[c : c + 1, :].astype(F32)
        chunks.append(part.astype(BF16))
    normed = jnp.concatenate(chunks, axis=1)
    l_wq.wait()
    query = jnp.dot(normed, wq[...], preferred_element_type=F32).astype(BF16).astype(F32)
    query = rotate(query).astype(BF16)
    qbuf[me] = query

    pl.semaphore_wait(barrier, N - 1)
    q_copies = [send(0, qbuf.at[me], qbuf.at[me], peer) for peer in peers]

    l_wk.wait()
    l_wv.wait()
    key_part = dot_rows(normed, wk[...]).astype(BF16)
    value_part = dot_rows(normed, wv[...]).astype(BF16)
    quarter = HEAD_DIM // GROUP
    place = lax.broadcasted_iota(jnp.int32, (quarter, HEAD_DIM), 1)
    origin = lax.broadcasted_iota(jnp.int32, (quarter, HEAD_DIM), 0)
    member = lax.rem(me, GROUP)
    spread = jnp.where(place == origin + member * quarter, 1.0, 0.0).astype(BF16)
    kvbuf[0, 0] = jnp.dot(key_part, spread, preferred_element_type=F32).astype(BF16)
    kvbuf[0, 1] = jnp.dot(value_part, spread, preferred_element_type=F32).astype(BF16)
    mates = [me - member + lax.rem(member + k, GROUP) for k in range(1, GROUP)]
    kv_copies = []
    for k, peer in enumerate(mates, 1):
        copy = pltpu.make_async_remote_copy(
            src_ref=kvbuf.at[0], dst_ref=kvbuf.at[k], send_sem=kv_send.at[k], recv_sem=kv_recv.at[k],
            device_id={"cache": peer}, device_id_type=MESH,
        )
        copy.start()
        kv_copies.append(copy)

    rows = GROUP * seqs
    row4 = lax.broadcasted_iota(jnp.int32, (rows, HEAD_DIM), 0)
    pick = [jnp.where(lax.rem(row4, seqs) == s, 1.0, 0.0).astype(BF16) for s in range(seqs)]
    valid4 = jnp.concatenate([valid] * GROUP, axis=0)
    lane4 = lax.rem(lax.broadcasted_iota(jnp.int32, (rows, HEAD_DIM), 1), 4)

    def attend(g):
        cols = pl.ds(pl.multiple_of(g * HEAD_DIM, HEAD_DIM), HEAD_DIM)
        qg = qbuf[pl.ds(g * GROUP, GROUP)].reshape(rows, HEAD_DIM)
        left = jnp.concatenate([qg * pick[s] for s in range(seqs)], axis=1)
        keys = jnp.concatenate([kc[s, :, cols] for s in range(seqs)], axis=1)
        scores = dot_rows(left, keys)
        scores = jnp.where(valid4, scores * (1.0 / math.sqrt(HEAD_DIM)), LOW)
        top = jnp.max(scores, axis=-1, keepdims=True)
        weights = jnp.where(valid4, jnp.exp(scores - top), 0.0)
        total = row_sum(weights)
        low = weights.astype(BF16)
        left = jnp.concatenate([low * pick[s] for s in range(seqs)], axis=1)
        values = jnp.concatenate([vc[s, :, cols] for s in range(seqs)], axis=0)
        summed = jnp.dot(left, values, preferred_element_type=F32)
        some = total > 0.0
        safe = jnp.where(some, total, 1.0)
        share = (summed * (1.0 / safe)).astype(BF16)
        level = jnp.broadcast_to(jnp.where(some, top + jnp.log(safe), LOW), (rows, HEAD_DIM))
        high, mid, low3 = split3(level)
        stat = jnp.where(
            lane4 == 0, high.astype(F32),
            jnp.where(lane4 == 1, mid.astype(F32), jnp.where(lane4 == 2, low3.astype(F32), 0.0)),
        ).astype(BF16)
        osend[pl.ds(g * GROUP, GROUP), 0] = share.reshape(GROUP, seqs, HEAD_DIM)
        osend[pl.ds(g * GROUP, GROUP), 1] = stat.reshape(GROUP, seqs, HEAD_DIM)

    side = z // GROUP

    def group_at(dy, ds):
        return lax.rem(y + dy, NY) * 2 + lax.rem(side + ds, 2)

    def members(dy, ds):
        if (dy, ds) == (0, 0):
            return mates
        return [group_at(dy, ds) * GROUP + j for j in range(GROUP)]

    l_kc.wait()
    l_vc.wait()
    o_copies = []
    for batch in BATCHES:
        for dy, ds in batch:
            for peer in members(dy, ds):
                arrived(0, qbuf.at[peer], peer)
        for dy, ds in batch:
            attend(group_at(dy, ds))
        for dy, ds in reversed(batch):
            for peer in members(dy, ds):
                o_copies.append(send(1, osend.at[peer], orecv.at[me], peer))
    sent(q_copies)

    for copy in kv_copies:
        copy.wait_recv()
    key_raw = kvbuf[0, 0].astype(F32)
    value_new = kvbuf[0, 1].astype(F32)
    for k in range(1, GROUP):
        key_raw = key_raw + kvbuf[k, 0].astype(F32)
        value_new = value_new + kvbuf[k, 1].astype(F32)
    key_new = rotate(key_raw).astype(BF16).astype(F32)
    own = row_sum(qbuf[me].astype(F32) * key_new) * (1.0 / math.sqrt(HEAD_DIM))
    own = jnp.broadcast_to(own, (seqs, HEAD_DIM))
    sent(kv_copies)
    l_wo.wait()
    l_mgain.wait()
    l_wg.wait()
    l_wu.wait()
    l_wd.wait()
    mgain_wide[...] = mgain[...].astype(F32)

    def level_of(stat):
        pair = stat + pltpu.roll(stat, 1, 1)
        return pair + pltpu.roll(pair, 2, 1)

    def merge(state, parts):
        peak, weight_sum, number = state
        levels = [level_of(ref[1].astype(F32)) for ref in parts]
        top = peak
        for level in levels:
            top = jnp.maximum(top, level)
        factor = jnp.exp(peak - top)
        weight_sum = weight_sum * factor
        number = number * factor
        for level, ref in zip(levels, parts):
            factor = jnp.exp(level - top)
            weight_sum = weight_sum + factor
            number = number + factor * ref[0].astype(F32)
        return top, weight_sum, number

    state = merge((own, jnp.ones((seqs, HEAD_DIM), F32), value_new), [osend.at[me]])
    for least, most in ((0, 3), (4, 4), (5, 6)):
        near = [p for p, d in zip(peers, DISTANCE) if least <= d <= most]
        for peer in near:
            arrived(1, orecv.at[peer], peer)
        state = merge(state, [orecv.at[peer] for peer in near])
    attended = (state[2] / state[1]).astype(BF16)

    def scatter(phase, left, weight, stage, landing):
        copies = []
        order = peers + [me]
        for first in range(0, N, 8):
            part_of = order[first : first + 8]
            for p in part_of:
                cols = pl.ds(pl.multiple_of(p * 128, 128), 128)
                stage[p] = jnp.dot(left, weight[:, cols], preferred_element_type=F32).astype(BF16)
            for p in part_of:
                if p is not me:
                    copies.append(send(phase, stage.at[p], landing.at[me], p))
        return copies

    def gathered(phase, stage, landing):
        total = stage[me].astype(F32)
        for peer in reversed(peers):
            arrived(phase, landing.at[peer], peer)
            total = total + landing[peer].astype(F32)
        return total

    p_copies = scatter(2, attended, wo, psend, precv)
    sent(o_copies)
    mine = pl.ds(pl.multiple_of(me * 128, 128), 128)
    mid_own = (hidden[:, mine].astype(F32) + gathered(2, psend, precv)).astype(BF16)
    midbuf[me] = mid_own
    m_copies = [send(3, midbuf.at[me], midbuf.at[me], peer) for peer in peers]
    sent(p_copies)

    squares = jnp.zeros((seqs, 128), F32)
    gate = jnp.zeros((seqs, wg.shape[0]), F32)
    upper = jnp.zeros((seqs, wg.shape[0]), F32)
    for least, most in ((0, 2), (3, 3), (4, 4), (5, 6)):
        near = [p for p, d in zip(peers, DISTANCE) if least <= d <= most]
        for peer in near:
            arrived(3, midbuf.at[peer], peer)
        if least == 0:
            near = near + [me]
        parts = []
        for peer in near:
            part = midbuf[peer].astype(F32)
            squares = squares + part * part
            parts.append((part * mgain_wide[pl.ds(peer, 1), :]).astype(BF16))
        left = jnp.concatenate(parts, axis=1)
        places = [pl.ds(pl.multiple_of(p * 128, 128), 128) for p in near]
        gate = gate + dot_rows(left, jnp.concatenate([wg[:, c] for c in places], axis=1))
        upper = upper + dot_rows(left, jnp.concatenate([wu[:, c] for c in places], axis=1))
    scale = lax.rsqrt(row_sum(squares) / width + 1e-5)
    gate = gate * scale
    act = (gate / (1.0 + jnp.exp(-gate)) * (upper * scale)).astype(BF16)
    d_copies = scatter(4, act, wd, dsend, drecv)
    sent(m_copies)
    total = gathered(4, dsend, drecv)
    out_ref[...] = (mid_own.astype(F32) + total).astype(BF16)
    sent(d_copies)


def per_device(*args):
    (hidden_in, attn_gain, w_query, w_key, w_value, key_cache, value_cache, write_pos, cache_len, w_out, mlp_gain,
     w_gate, w_up, w_down) = args
    seqs, width = hidden_in.shape
    lines = width // 128
    attn_gain = attn_gain.reshape(lines, 128)
    mlp_gain = mlp_gain.reshape(lines, 128)
    w_key, w_value, w_gate, w_up = w_key.T, w_value.T, w_gate.T, w_up.T
    operands = (hidden_in, attn_gain, w_query, w_key, w_value, key_cache, value_cache, write_pos, cache_len, w_out,
                mlp_gain, w_gate, w_up, w_down)
    held = [pltpu.VMEM(a.shape, a.dtype) for a in operands]
    held[7] = pltpu.SMEM(write_pos.shape, write_pos.dtype)
    held[8] = pltpu.SMEM(cache_len.shape, cache_len.dtype)
    block = (N, seqs, 128)
    return pl.pallas_call(
        kernel,
        out_shape=jax.ShapeDtypeStruct((seqs, 128), BF16),
        in_specs=[pl.BlockSpec(memory_space=pltpu.HBM)] * len(operands),
        out_specs=pl.BlockSpec(memory_space=pltpu.VMEM),
        scratch_shapes=held
        + [
            pltpu.VMEM(block, BF16),
            pltpu.VMEM((GROUP, 2, seqs, 128), BF16),
            pltpu.VMEM((N, 2, seqs, 128), BF16),
            pltpu.VMEM((N, 2, seqs, 128), BF16),
            pltpu.VMEM(block, BF16),
            pltpu.VMEM(block, BF16),
            pltpu.VMEM(block, BF16),
            pltpu.VMEM(block, BF16),
            pltpu.VMEM(block, BF16),
            pltpu.VMEM((lines, 128), F32),
            pltpu.SemaphoreType.DMA((len(operands),)),
            pltpu.SemaphoreType.DMA((5, N)),
            pltpu.SemaphoreType.DMA((5, N)),
            pltpu.SemaphoreType.DMA((GROUP,)),
            pltpu.SemaphoreType.DMA((GROUP,)),
        ],
        compiler_params=pltpu.CompilerParams(
            collective_id=0, has_side_effects=True, vmem_limit_bytes=67043328
        ),
    )(*operands)


def solution(mesh):
    in_specs = (
        P("batch", None),
        P(),
        P(None, "cache"),
        P(None, "cache"),
        P(None, "cache"),
        P("batch", "cache", None),
        P("batch", "cache", None),
        P("batch"),
        P("batch"),
        P("cache", None),
        P(),
        P(None, "cache"),
        P(None, "cache"),
        P("cache", None),
    )
    return jax.shard_map(
        per_device, mesh=mesh, in_specs=in_specs, out_specs=P("batch", "cache"), check_vma=False
    )
```

time: 49.7 us -> 47.2 us (0.950)
  Pallas kernels: 48.4 us -> 45.8 us
    pallas_call x1, Pallas kernels: 48.4 us -> 45.8 us  [per_device(): pl.pallas_call(kernel, out_shape=jax.ShapeDtypeStruct((seqs, 128), BF16),...]
where the time goes in v2:
time: 47.2 us; the launch traced here: 47.1 us
  Pallas kernels  45.8 us (97%)
  local copies, waits for them, and re-layouts  1.26 us (3%)
    pallas_call x1, Pallas kernels, per_device(): pl.pallas_call(kernel, out_shape=jax.ShapeDtypeStruct((seqs, 128), BF16),...  45.8 us
    unnamed x1, local copies, waits for them, and re-layouts  1.26 us

profile of v2, /device:TPU:6, one launch (start us, length us, event | category | flops | bytes accessed | tf_op | source)
XLA Modules:
  0.0 47.1 jit_solution(1725373826176780050)
XLA Ops:
  0.0 45.8 %shard_map.136 = bf16[8,128]{1,0:T(8,128)(2,1)} custom-call(bf16[8,4096]{1,0:T(8,128)(2,1)} %hidden_hbm.1, bf16[32,128]{1,0:T(8,128)(2,1)} %bitcast.10, bf16[4096,128]{1,0:T(8,128)(2,1)} %wq_hbm.1, bf16[32,4096]{1,0:T(8,128)(2,1)} %bitcast.8, bf16[32,4096]{1,0:T(8,128)(2,1)} %bitcast.9, bf16[8,128,1024]{2,1,0:T(8,128)(2,1)} %kc_hbm.1, ...), custom_call_target="tpu_custom_call" | custom-call | tf_op jit(solution)/shard_map/pallas_call | solution.py:325
  45.8 1.3 %copy.16 = bf16[8,128]{1,0:T(8,128)(2,1)} copy(bf16[8,128]{1,0:T(8,128)(2,1)} %shard_map.136) | data formatting | bytes 4096

commit v3 on v2

v3 whole, which is shorter than its diff:
```python
import functools
import math

import jax
import jax.numpy as jnp
from jax import lax
from jax.experimental import pallas as pl
from jax.experimental.pallas import tpu as pltpu
from jax.sharding import PartitionSpec as P

HEADS = 32
KV_HEADS = 8
HEAD_DIM = 128
GROUP = HEADS // KV_HEADS
NY, NZ = 4, 8
N = NY * NZ
LOW = -1e30
MESH = pl.DeviceIdType.MESH
F32 = jnp.float32
BF16 = jnp.bfloat16

OFFSETS = sorted(
    [(dy, dz) for dy in range(NY) for dz in range(NZ) if (dy, dz) != (0, 0)],
    key=lambda t: -(min(t[0], NY - t[0]) + min(t[1], NZ - t[1])),
)
DISTANCE = [min(dy, NY - dy) + min(dz, NZ - dz) for dy, dz in OFFSETS]
MID_CLASSES = ((1, 2), (3, 3), (4, 4), (5, 6))
NEAR = 4
BATCHES = (((0, 0), (0, 1), (1, 0), (3, 0)), ((1, 1), (3, 1), (2, 0)), ((2, 1),))


def mid_class(distance):
    return [least <= distance <= most for least, most in MID_CLASSES].index(True)


def row_sum(x):
    return jnp.sum(x, axis=-1, keepdims=True)


def dot_rows(a, b):
    return lax.dot_general(a, b, (((1,), (1,)), ((), ())), preferred_element_type=F32)


def split3(x):
    high = x.astype(BF16)
    rest = x - high.astype(F32)
    mid = rest.astype(BF16)
    low = (rest - mid.astype(F32)).astype(BF16)
    return high, mid, low


def kernel(
    hidden_hbm, gain_hbm, wq_hbm, wk_hbm, wv_hbm, kc_hbm, vc_hbm, pos_hbm, len_hbm,
    wo_hbm, mgain_hbm, wg_hbm, wu_hbm, wd_hbm,
    out_ref,
    hidden, gain, wq, wk, wv, kc, vc, pos_ref, len_ref, wo, mgain, wg, wu, wd,
    qbuf, kvbuf, osend, orecv, psend, precv, midbuf, dsend, drecv, mgain_wide,
    load_sem, send_sem, q_sem, kv_sem, o_sem, p_sem, m_sem, d_sem,
):
    me = lax.axis_index("cache")
    y, z = lax.shift_right_logical(me, 3), jnp.bitwise_and(me, NZ - 1)
    seqs = hidden.shape[0]
    width = hidden.shape[1]
    slots = kc.shape[2]

    rows_at = [jnp.bitwise_and(y + dy, NY - 1) * NZ for dy in range(NY)]
    cols_at = [jnp.bitwise_and(z + dz, NZ - 1) for dz in range(NZ)]
    peers = [rows_at[dy] + cols_at[dz] for dy, dz in OFFSETS]

    def at_distance(least, most):
        return [p for p, d in zip(peers, DISTANCE) if least <= d <= most]

    barrier = pltpu.get_barrier_semaphore()
    for peer in peers:
        pl.semaphore_signal(barrier, inc=1, device_id={"cache": peer}, device_id_type=MESH)

    def block(c):
        return pl.ds(pl.multiple_of(c * 128, 128), 128)

    plain = [
        (hidden_hbm, hidden), (gain_hbm, gain), (pos_hbm, pos_ref), (len_hbm, len_ref), (wq_hbm, wq), (wk_hbm, wk),
        (wv_hbm, wv), (mgain_hbm, mgain),
    ]
    loads = [pltpu.make_async_copy(a, b, load_sem.at[i]) for i, (a, b) in enumerate(plain)]
    for copy in loads:
        copy.start()
    l_hidden, l_gain, l_pos, l_len, l_wq, l_wk, l_wv, l_mgain = loads
    first = len(plain)
    for g in range(KV_HEADS):
        pltpu.make_async_copy(kc_hbm.at[:, :, block(g)], kc.at[g], load_sem.at[first]).start()
    for g in range(KV_HEADS):
        pltpu.make_async_copy(vc_hbm.at[:, :, block(g)], vc.at[g], load_sem.at[first + 1]).start()
    weights = ((wo_hbm, wo), (wg_hbm, wg), (wu_hbm, wu), (wd_hbm, wd))

    def load_weights(c, _):
        for i, (a, b) in enumerate(weights):
            pltpu.make_async_copy(a.at[:, block(c)], b.at[c], load_sem.at[first + 2 + i]).start()
        return 0

    def loaded(i, ref):
        pltpu.make_async_copy(ref, ref, load_sem.at[first + i]).wait()

    def send(phase, src, dst, recv_sem, peer):
        pltpu.make_async_remote_copy(
            src_ref=src, dst_ref=dst, send_sem=send_sem.at[phase], recv_sem=recv_sem,
            device_id={"cache": peer}, device_id_type=MESH,
        ).start()

    def pending(phase, ref, recv_sem):
        return pltpu.make_async_remote_copy(
            src_ref=ref, dst_ref=ref, send_sem=send_sem.at[phase], recv_sem=recv_sem,
            device_id={"cache": peers[0]}, device_id_type=MESH,
        )

    def arrived(recv_sem, ref):
        pending(0, ref, recv_sem).wait_recv()

    def sent(phase, ref):
        pending(phase, ref, kv_sem.at[0]).wait_send()

    def some(buffer, count):
        return buffer.at[pl.ds(0, count)]

    lane = lax.broadcasted_iota(jnp.int32, (seqs, HEAD_DIM), 1)
    row = lax.broadcasted_iota(jnp.int32, (seqs, HEAD_DIM), 0)
    half = HEAD_DIM // 2
    l_pos.wait()
    l_len.wait()
    pos = jnp.zeros((seqs, HEAD_DIM), jnp.int32)
    length = jnp.zeros((seqs, HEAD_DIM), jnp.int32)
    for s in range(seqs):
        pos = jnp.where(row == s, pos_ref[s], pos)
        length = jnp.where(row == s, len_ref[s], length)
    freq = jnp.exp(lax.rem(lane, half).astype(F32) * (-math.log(10000.0) / half))
    angle = pos.astype(F32) * freq
    cosine = jnp.cos(angle)
    sine = jnp.sin(angle) * jnp.where(lane < half, -1.0, 1.0)

    def rotate(x):
        return x * cosine + pltpu.roll(x, half, 1) * sine

    slot = me * slots + lane
    dist = jnp.bitwise_and(pos - 1 - slot, slots * N - 1) + 1
    valid = dist <= length

    l_hidden.wait()
    l_gain.wait()
    wide = hidden[...].astype(F32)
    scale = lax.rsqrt(row_sum(wide * wide) / width + 1e-5)
    chunks = []
    for c in range(width // 128):
        part = wide[:, c * 128 : (c + 1) * 128] * scale * gain[c : c + 1, :].astype(F32)
        chunks.append(part.astype(BF16))
    normed = jnp.concatenate(chunks, axis=1)
    l_wq.wait()
    query = jnp.dot(normed, wq[...], preferred_element_type=F32).astype(BF16).astype(F32)
    query = rotate(query).astype(BF16)
    qbuf[me] = query

    pl.semaphore_wait(barrier, N - 1)
    home = lax.shift_right_logical(me, 2)
    for peer in peers:
        send(0, qbuf.at[me], qbuf.at[me], q_sem.at[home], peer)
    lax.fori_loop(0, N, load_weights, 0)

    l_wk.wait()
    l_wv.wait()
    key_part = dot_rows(normed, wk[...]).astype(BF16)
    value_part = dot_rows(normed, wv[...]).astype(BF16)
    quarter = HEAD_DIM // GROUP
    place = lax.broadcasted_iota(jnp.int32, (quarter, HEAD_DIM), 1)
    origin = lax.broadcasted_iota(jnp.int32, (quarter, HEAD_DIM), 0)
    member = jnp.bitwise_and(me, GROUP - 1)
    spread = jnp.where(place == origin + member * quarter, 1.0, 0.0).astype(BF16)
    kvbuf[0, 0] = jnp.dot(key_part, spread, preferred_element_type=F32).astype(BF16)
    kvbuf[0, 1] = jnp.dot(value_part, spread, preferred_element_type=F32).astype(BF16)
    for k in range(1, GROUP):
        peer = me - member + jnp.bitwise_and(member + k, GROUP - 1)
        send(5, kvbuf.at[0], kvbuf.at[k], kv_sem.at[0], peer)

    rows = GROUP * seqs
    row4 = lax.broadcasted_iota(jnp.int32, (rows, HEAD_DIM), 0)
    pick = [jnp.where(lax.rem(row4, seqs) == s, 1.0, 0.0).astype(BF16) for s in range(seqs)]
    valid4 = jnp.concatenate([valid] * GROUP, axis=0)
    lane4 = lax.rem(lax.broadcasted_iota(jnp.int32, (rows, HEAD_DIM), 1), 4)

    def attend(g):
        qg = qbuf[pl.ds(g * GROUP, GROUP)].reshape(rows, HEAD_DIM)
        left = jnp.concatenate([qg * pick[s] for s in range(seqs)], axis=1)
        keys = jnp.concatenate([kc[g, s] for s in range(seqs)], axis=1)
        scores = dot_rows(left, keys)
        scores = jnp.where(valid4, scores * (1.0 / math.sqrt(HEAD_DIM)), LOW)
        top = jnp.max(scores, axis=-1, keepdims=True)
        weights = jnp.where(valid4, jnp.exp(scores - top), 0.0)
        total = row_sum(weights)
        low = weights.astype(BF16)
        left = jnp.concatenate([low * pick[s] for s in range(seqs)], axis=1)
        values = vc[g].reshape(seqs * slots, HEAD_DIM)
        summed = jnp.dot(left, values, preferred_element_type=F32)
        any_slot = total > 0.0
        safe = jnp.where(any_slot, total, 1.0)
        share = (summed * (1.0 / safe)).astype(BF16)
        level = jnp.broadcast_to(jnp.where(any_slot, top + jnp.log(safe), LOW), (rows, HEAD_DIM))
        high, mid, low3 = split3(level)
        stat = jnp.where(
            lane4 == 0, high.astype(F32),
            jnp.where(lane4 == 1, mid.astype(F32), jnp.where(lane4 == 2, low3.astype(F32), 0.0)),
        ).astype(BF16)
        osend[pl.ds(g * GROUP, GROUP), 0] = share.reshape(GROUP, seqs, HEAD_DIM)
        osend[pl.ds(g * GROUP, GROUP), 1] = stat.reshape(GROUP, seqs, HEAD_DIM)

    side = lax.shift_right_logical(z, 2)
    sides = [side, 1 - side]

    def group_at(dy, ds):
        return lax.shift_right_logical(rows_at[dy], 2) + sides[ds]

    loaded(0, kc)
    loaded(1, vc)
    for batch in BATCHES:
        for dy, ds in batch:
            g = group_at(dy, ds)
            arrived(q_sem.at[g], some(qbuf, GROUP - 1 if (dy, ds) == (0, 0) else GROUP))
        for dy, ds in batch:
            attend(group_at(dy, ds))
        for dy, ds in reversed(batch):
            for j in range(GROUP):
                if (dy, ds) == (0, 0):
                    if j == 0:
                        continue
                    peer = me - member + jnp.bitwise_and(member + j, GROUP - 1)
                else:
                    peer = group_at(dy, ds) * GROUP + j
                send(1, osend.at[peer], orecv.at[me], o_sem.at[home], peer)
    sent(0, some(qbuf, N - 1))

    arrived(kv_sem.at[0], some(kvbuf, GROUP - 1))
    key_raw = kvbuf[0, 0].astype(F32)
    value_new = kvbuf[0, 1].astype(F32)
    for k in range(1, GROUP):
        key_raw = key_raw + kvbuf[k, 0].astype(F32)
        value_new = value_new + kvbuf[k, 1].astype(F32)
    key_new = rotate(key_raw).astype(BF16).astype(F32)
    own = row_sum(qbuf[me].astype(F32) * key_new) * (1.0 / math.sqrt(HEAD_DIM))
    own = jnp.broadcast_to(own, (seqs, HEAD_DIM))
    for i, (_, ref) in enumerate(weights):
        loaded(2 + i, ref)
    l_mgain.wait()
    mgain_wide[...] = mgain[...].astype(F32)

    def level_of(stat):
        pair = stat + pltpu.roll(stat, 1, 1)
        return pair + pltpu.roll(pair, 2, 1)

    def merge(state, parts):
        peak, weight_sum, number = state
        levels = [level_of(ref[1].astype(F32)) for ref in parts]
        top = peak
        for level in levels:
            top = jnp.maximum(top, level)
        factor = jnp.exp(peak - top)
        weight_sum = weight_sum * factor
        number = number * factor
        for level, ref in zip(levels, parts):
            factor = jnp.exp(level - top)
            weight_sum = weight_sum + factor
            number = number + factor * ref[0].astype(F32)
        return top, weight_sum, number

    state = merge((own, jnp.ones((seqs, HEAD_DIM), F32), value_new), [osend.at[me]])
    for batch in BATCHES:
        parts = []
        for dy, ds in batch:
            g = group_at(dy, ds)
            if (dy, ds) == (0, 0):
                arrived(o_sem.at[g], some(orecv, GROUP - 1))
                parts += [orecv.at[me - member + jnp.bitwise_and(member + k, GROUP - 1)] for k in range(1, GROUP)]
            else:
                arrived(o_sem.at[g], some(orecv, GROUP))
                parts += [orecv.at[g * GROUP + j] for j in range(GROUP)]
        state = merge(state, parts)
    sent(1, some(osend, N - 1))
    sent(5, some(kvbuf, GROUP - 1))
    attended = (state[2] / state[1]).astype(BF16)

    def scatter(phase, left, weight, stage, landing, recv_sem):
        order = peers + [me]
        far = [d > NEAR for d in DISTANCE] + [False]
        for first in range(0, N, 8):
            part_of = order[first : first + 8]
            for p in part_of:
                stage[p] = jnp.dot(left, weight[p], preferred_element_type=F32).astype(BF16)
            for i, p in enumerate(part_of, first):
                if i < N - 1:
                    send(phase, stage.at[p], landing.at[me], recv_sem.at[int(far[i])], p)

    def gathered(stage, landing, recv_sem):
        total = stage[me].astype(F32)
        for i, (least, most) in enumerate(((1, NEAR), (NEAR + 1, NY + NZ))):
            near = at_distance(least, most)
            arrived(recv_sem.at[i], some(landing, len(near)))
            parts = [landing[p].astype(F32) for p in near]
            while len(parts) > 1:
                parts = [sum(parts[j : j + 2]) for j in range(0, len(parts), 2)]
            total = total + parts[0]
        return total

    scatter(2, attended, wo, psend, precv, p_sem)
    mid_own = (hidden[:, block(me)].astype(F32) + gathered(psend, precv, p_sem)).astype(BF16)
    midbuf[me] = mid_own
    for peer, d in zip(peers, DISTANCE):
        send(3, midbuf.at[me], midbuf.at[me], m_sem.at[mid_class(d)], peer)
    sent(2, some(psend, N - 1))

    squares = jnp.zeros((seqs, 128), F32)
    gate = jnp.zeros((seqs, wg.shape[1]), F32)
    upper = jnp.zeros((seqs, wg.shape[1]), F32)
    for i, (least, most) in enumerate(MID_CLASSES):
        near = at_distance(least, most)
        arrived(m_sem.at[i], some(midbuf, len(near)))
        if i == 0:
            near = near + [me]
        parts = []
        for peer in near:
            part = midbuf[peer].astype(F32)
            squares = squares + part * part
            parts.append((part * mgain_wide[pl.ds(peer, 1), :]).astype(BF16))
        left = jnp.concatenate(parts, axis=1)
        gate = gate + dot_rows(left, jnp.concatenate([wg[p] for p in near], axis=1))
        upper = upper + dot_rows(left, jnp.concatenate([wu[p] for p in near], axis=1))
    scale = lax.rsqrt(row_sum(squares) / width + 1e-5)
    gate = gate * scale
    act = (gate / (1.0 + jnp.exp(-gate)) * (upper * scale)).astype(BF16)
    scatter(4, act, wd, dsend, drecv, d_sem)
    sent(3, some(midbuf, N - 1))
    total = gathered(dsend, drecv, d_sem)
    out_ref[...] = (mid_own.astype(F32) + total).astype(BF16)
    sent(4, some(dsend, N - 1))


def per_device(*args):
    (hidden_in, attn_gain, w_query, w_key, w_value, key_cache, value_cache, write_pos, cache_len, w_out, mlp_gain,
     w_gate, w_up, w_down) = args
    seqs, width = hidden_in.shape
    lines = width // 128
    attn_gain = attn_gain.reshape(lines, 128)
    mlp_gain = mlp_gain.reshape(lines, 128)
    w_key, w_value, w_gate, w_up = w_key.T, w_value.T, w_gate.T, w_up.T
    operands = (hidden_in, attn_gain, w_query, w_key, w_value, key_cache, value_cache, write_pos, cache_len, w_out,
                mlp_gain, w_gate, w_up, w_down)
    held = [pltpu.VMEM(a.shape, a.dtype) for a in operands]
    held[7] = pltpu.SMEM(write_pos.shape, write_pos.dtype)
    held[8] = pltpu.SMEM(cache_len.shape, cache_len.dtype)
    for i in (5, 6):
        held[i] = pltpu.VMEM((KV_HEADS, *key_cache.shape[:2], HEAD_DIM), key_cache.dtype)
    for i in (9, 11, 12, 13):
        held[i] = pltpu.VMEM((lines, operands[i].shape[0], 128), operands[i].dtype)
    block = (N, seqs, 128)
    return pl.pallas_call(
        kernel,
        out_shape=jax.ShapeDtypeStruct((seqs, 128), BF16),
        in_specs=[pl.BlockSpec(memory_space=pltpu.HBM)] * len(operands),
        out_specs=pl.BlockSpec(memory_space=pltpu.VMEM),
        scratch_shapes=held
        + [
            pltpu.VMEM(block, BF16),
            pltpu.VMEM((GROUP, 2, seqs, 128), BF16),
            pltpu.VMEM((N, 2, seqs, 128), BF16),
            pltpu.VMEM((N, 2, seqs, 128), BF16),
            pltpu.VMEM(block, BF16),
            pltpu.VMEM(block, BF16),
            pltpu.VMEM(block, BF16),
            pltpu.VMEM(block, BF16),
            pltpu.VMEM(block, BF16),
            pltpu.VMEM((lines, 128), F32),
            pltpu.SemaphoreType.DMA((len(operands),)),
            pltpu.SemaphoreType.DMA((6,)),
            pltpu.SemaphoreType.DMA((KV_HEADS,)),
            pltpu.SemaphoreType.DMA((1,)),
            pltpu.SemaphoreType.DMA((KV_HEADS,)),
            pltpu.SemaphoreType.DMA((2,)),
            pltpu.SemaphoreType.DMA((len(MID_CLASSES),)),
            pltpu.SemaphoreType.DMA((2,)),
        ],
        compiler_params=pltpu.CompilerParams(
            collective_id=0, has_side_effects=True, vmem_limit_bytes=67043328
        ),
    )(*operands)


def solution(mesh):
    in_specs = (
        P("batch", None),
        P(),
        P(None, "cache"),
        P(None, "cache"),
        P(None, "cache"),
        P("batch", "cache", None),
        P("batch", "cache", None),
        P("batch"),
        P("batch"),
        P("cache", None),
        P(),
        P(None, "cache"),
        P(None, "cache"),
        P("cache", None),
    )
    return jax.shard_map(
        per_device, mesh=mesh, in_specs=in_specs, out_specs=P("batch", "cache"), check_vma=False
    )
```

time: 47.2 us -> 44.3 us (0.939)
  Pallas kernels: 45.8 us -> 43 us
    pallas_call x1, Pallas kernels: 45.8 us -> 43 us  [per_device(): pl.pallas_call(kernel, out_shape=jax.ShapeDtypeStruct((seqs, 128), BF16),...]
where the time goes in v3:
time: 44.3 us; the launch traced here: 44.2 us
  Pallas kernels  43 us (97%)
  local copies, waits for them, and re-layouts  1.26 us (3%)
    pallas_call x1, Pallas kernels, per_device(): pl.pallas_call(kernel, out_shape=jax.ShapeDtypeStruct((seqs, 128), BF16),...  43 us
    unnamed x1, local copies, waits for them, and re-layouts  1.26 us

profile of v3, /device:TPU:6, one launch (start us, length us, event | category | flops | bytes accessed | tf_op | source)
XLA Modules:
  0.0 44.2 jit_solution(14567273256526469661)
XLA Ops:
  0.0 43.0 %shard_map.136 = bf16[8,128]{1,0:T(8,128)(2,1)} custom-call(bf16[8,4096]{1,0:T(8,128)(2,1)} %hidden_hbm.1, bf16[32,128]{1,0:T(8,128)(2,1)} %bitcast.10, bf16[4096,128]{1,0:T(8,128)(2,1)} %wq_hbm.1, bf16[32,4096]{1,0:T(8,128)(2,1)} %bitcast.8, bf16[32,4096]{1,0:T(8,128)(2,1)} %bitcast.9, bf16[8,128,1024]{2,1,0:T(8,128)(2,1)} %kc_hbm.1, ...), custom_call_target="tpu_custom_call" | custom-call | tf_op jit(solution)/shard_map/pallas_call | solution.py:359
  43.0 1.3 %copy.16 = bf16[8,128]{1,0:T(8,128)(2,1)} copy(bf16[8,128]{1,0:T(8,128)(2,1)} %shard_map.136) | data formatting | bytes 4096

commit v4 on v3

--- a/solution.py
+++ b/solution.py
@@ -24,9 +24,17 @@
     key=lambda t: -(min(t[0], NY - t[0]) + min(t[1], NZ - t[1])),
 )
 DISTANCE = [min(dy, NY - dy) + min(dz, NZ - dz) for dy, dz in OFFSETS]
-MID_CLASSES = ((1, 2), (3, 3), (4, 4), (5, 6))
 NEAR = 4
-BATCHES = (((0, 0), (0, 1), (1, 0), (3, 0)), ((1, 1), (3, 1), (2, 0)), ((2, 1),))
+PAIRS = sorted(
+    [(dy, dz) for dy in range(NY) for dz in range(NZ // 2)],
+    key=lambda t: -(min(t[0], NY - t[0]) + max(t[1], NZ // 2 - t[1])),
+)
+MID_OFFSETS = sorted(
+    [(dy, dz) for dy in range(NY) for dz in (7, 0, 1, 2) if (dy, dz) != (0, 0)],
+    key=lambda t: -(min(t[0], NY - t[0]) + min(t[1], NZ - t[1])),
+)
+MID_DISTANCE = [min(dy, NY - dy) + min(dz, NZ - dz) for dy, dz in MID_OFFSETS]
+MID_CLASSES = ((1, 2), (3, 3), (4, 4))
 
 
 def mid_class(distance):
@@ -54,7 +62,7 @@
     wo_hbm, mgain_hbm, wg_hbm, wu_hbm, wd_hbm,
     out_ref,
     hidden, gain, wq, wk, wv, kc, vc, pos_ref, len_ref, wo, mgain, wg, wu, wd,
-    qbuf, kvbuf, osend, orecv, psend, precv, midbuf, dsend, drecv, mgain_wide,
+    qbuf, kvbuf, osend, orecv, psend, precv, midbuf, dsend, drecv, mgain_wide, ktr, wgt, wut,
     load_sem, send_sem, q_sem, kv_sem, o_sem, p_sem, m_sem, d_sem,
 ):
     me = lax.axis_index("cache")
@@ -158,9 +166,8 @@
     qbuf[me] = query
 
     pl.semaphore_wait(barrier, N - 1)
-    home = lax.shift_right_logical(me, 2)
     for peer in peers:
-        send(0, qbuf.at[me], qbuf.at[me], q_sem.at[home], peer)
+        send(0, qbuf.at[me], qbuf.at[me], q_sem.at[0], peer)
     lax.fori_loop(0, N, load_weights, 0)
 
     l_wk.wait()
@@ -184,54 +191,50 @@
     valid4 = jnp.concatenate([valid] * GROUP, axis=0)
     lane4 = lax.rem(lax.broadcasted_iota(jnp.int32, (rows, HEAD_DIM), 1), 4)
 
-    def attend(g):
-        qg = qbuf[pl.ds(g * GROUP, GROUP)].reshape(rows, HEAD_DIM)
-        left = jnp.concatenate([qg * pick[s] for s in range(seqs)], axis=1)
-        keys = jnp.concatenate([kc[g, s] for s in range(seqs)], axis=1)
-        scores = dot_rows(left, keys)
-        scores = jnp.where(valid4, scores * (1.0 / math.sqrt(HEAD_DIM)), LOW)
-        top = jnp.max(scores, axis=-1, keepdims=True)
-        weights = jnp.where(valid4, jnp.exp(scores - top), 0.0)
-        total = row_sum(weights)
-        low = weights.astype(BF16)
-        left = jnp.concatenate([low * pick[s] for s in range(seqs)], axis=1)
-        values = vc[g].reshape(seqs * slots, HEAD_DIM)
-        summed = jnp.dot(left, values, preferred_element_type=F32)
-        any_slot = total > 0.0
-        safe = jnp.where(any_slot, total, 1.0)
-        share = (summed * (1.0 / safe)).astype(BF16)
-        level = jnp.broadcast_to(jnp.where(any_slot, top + jnp.log(safe), LOW), (rows, HEAD_DIM))
-        high, mid, low3 = split3(level)
-        stat = jnp.where(
-            lane4 == 0, high.astype(F32),
-            jnp.where(lane4 == 1, mid.astype(F32), jnp.where(lane4 == 2, low3.astype(F32), 0.0)),
-        ).astype(BF16)
-        osend[pl.ds(g * GROUP, GROUP), 0] = share.reshape(GROUP, seqs, HEAD_DIM)
-        osend[pl.ds(g * GROUP, GROUP), 1] = stat.reshape(GROUP, seqs, HEAD_DIM)
-
-    side = lax.shift_right_logical(z, 2)
-    sides = [side, 1 - side]
-
-    def group_at(dy, ds):
-        return lax.shift_right_logical(rows_at[dy], 2) + sides[ds]
+    def attend(groups):
+        scores = []
+        for g in groups:
+            qg = qbuf[pl.ds(g * GROUP, GROUP)].reshape(rows, HEAD_DIM)
+            left = jnp.concatenate([qg * pick[s] for s in range(seqs)], axis=1)
+            keys = ktr[g].reshape(seqs * HEAD_DIM, slots)
+            scores.append(jnp.dot(left, keys, preferred_element_type=F32))
+        shares, tops, totals = [], [], []
+        for score in scores:
+            score = jnp.where(valid4, score * (1.0 / math.sqrt(HEAD_DIM)), LOW)
+            top = jnp.max(score, axis=-1, keepdims=True)
+            weights = jnp.where(valid4, jnp.exp(score - top), 0.0)
+            tops.append(top)
+            totals.append(row_sum(weights))
+            shares.append(weights.astype(BF16))
+        for g, low, top, total in zip(groups, shares, tops, totals):
+            left = jnp.concatenate([low * pick[s] for s in range(seqs)], axis=1)
+            values = vc[g].reshape(seqs * slots, HEAD_DIM)
+            summed = jnp.dot(left, values, preferred_element_type=F32)
+            any_slot = total > 0.0
+            safe = jnp.where(any_slot, total, 1.0)
+            share = (summed * (1.0 / safe)).astype(BF16)
+            level = jnp.broadcast_to(jnp.where(any_slot, top + jnp.log(safe), LOW), (rows, HEAD_DIM))
+            high, mid, low3 = split3(level)
+            stat = jnp.where(
+                lane4 == 0, high.astype(F32),
+                jnp.where(lane4 == 1, mid.astype(F32), jnp.where(lane4 == 2, low3.astype(F32), 0.0)),
+            ).astype(BF16)
+            osend[pl.ds(g * GROUP, GROUP), 0] = share.reshape(GROUP, seqs, HEAD_DIM)
+            osend[pl.ds(g * GROUP, GROUP), 1] = stat.reshape(GROUP, seqs, HEAD_DIM)
 
     loaded(0, kc)
     loaded(1, vc)
-    for batch in BATCHES:
-        for dy, ds in batch:
-            g = group_at(dy, ds)
-            arrived(q_sem.at[g], some(qbuf, GROUP - 1 if (dy, ds) == (0, 0) else GROUP))
-        for dy, ds in batch:
-            attend(group_at(dy, ds))
-        for dy, ds in reversed(batch):
-            for j in range(GROUP):
-                if (dy, ds) == (0, 0):
-                    if j == 0:
-                        continue
-                    peer = me - member + jnp.bitwise_and(member + j, GROUP - 1)
-                else:
-                    peer = group_at(dy, ds) * GROUP + j
-                send(1, osend.at[peer], orecv.at[me], o_sem.at[home], peer)
+
+    def turn_keys(g, _):
+        for s in range(seqs):
+            ktr[g, s] = kc[g, s].T
+        return 0
+
+    lax.fori_loop(0, KV_HEADS, turn_keys, 0)
+    arrived(q_sem.at[0], some(qbuf, N - 1))
+    attend(range(KV_HEADS))
+    for peer, d in zip(peers, DISTANCE):
+        send(1, osend.at[peer], orecv.at[me], o_sem.at[int(d > NEAR)], peer)
     sent(0, some(qbuf, N - 1))
 
     arrived(kv_sem.at[0], some(kvbuf, GROUP - 1))
@@ -246,6 +249,13 @@
     for i, (_, ref) in enumerate(weights):
         loaded(2 + i, ref)
     l_mgain.wait()
+
+    def turn_weights(c, _):
+        wgt[c] = wg[c].T
+        wut[c] = wu[c].T
+        return 0
+
+    lax.fori_loop(0, N, turn_weights, 0)
     mgain_wide[...] = mgain[...].astype(F32)
 
     def level_of(stat):
@@ -268,17 +278,10 @@
         return top, weight_sum, number
 
     state = merge((own, jnp.ones((seqs, HEAD_DIM), F32), value_new), [osend.at[me]])
-    for batch in BATCHES:
-        parts = []
-        for dy, ds in batch:
-            g = group_at(dy, ds)
-            if (dy, ds) == (0, 0):
-                arrived(o_sem.at[g], some(orecv, GROUP - 1))
-                parts += [orecv.at[me - member + jnp.bitwise_and(member + k, GROUP - 1)] for k in range(1, GROUP)]
-            else:
-                arrived(o_sem.at[g], some(orecv, GROUP))
-                parts += [orecv.at[g * GROUP + j] for j in range(GROUP)]
-        state = merge(state, parts)
+    for i, (least, most) in enumerate(((1, NEAR), (NEAR + 1, NY + NZ))):
+        near = at_distance(least, most)
+        arrived(o_sem.at[i], some(orecv, len(near)))
+        state = merge(state, [orecv.at[p] for p in near])
     sent(1, some(osend, N - 1))
     sent(5, some(kvbuf, GROUP - 1))
     attended = (state[2] / state[1]).astype(BF16)
@@ -305,35 +308,66 @@
             total = total + parts[0]
         return total
 
-    scatter(2, attended, wo, psend, precv, p_sem)
-    mid_own = (hidden[:, block(me)].astype(F32) + gathered(psend, precv, p_sem)).astype(BF16)
-    midbuf[me] = mid_own
-    for peer, d in zip(peers, DISTANCE):
-        send(3, midbuf.at[me], midbuf.at[me], m_sem.at[mid_class(d)], peer)
-    sent(2, some(psend, N - 1))
+    def tree(parts):
+        while len(parts) > 1:
+            parts = [sum(parts[j : j + 2]) for j in range(0, len(parts), 2)]
+        return parts[0]
+
+    quad = jnp.bitwise_and(z, NZ // 2 - 1)
+    mine = lax.shift_right_logical(rows_at[0], 1) + quad
+    for first in range(0, len(PAIRS), 4):
+        part_of = PAIRS[first : first + 4]
+        for dy, dz in part_of:
+            column = rows_at[dy] + jnp.bitwise_and(z + dz, NZ // 2 - 1)
+            at = psend.at[lax.shift_right_logical(rows_at[dy], 1) + jnp.bitwise_and(z + dz, NZ // 2 - 1)]
+            for h in range(2):
+                part = jnp.dot(attended, wo[column + h * (NZ // 2)], preferred_element_type=F32).astype(BF16)
+                at[h] = part
+                if (dy, dz) == (0, 0):
+                    precv[me, h] = part
+        for dy, dz in part_of:
+            at = psend.at[lax.shift_right_logical(rows_at[dy], 1) + jnp.bitwise_and(z + dz, NZ // 2 - 1)]
+            for far in (dz, dz + NZ // 2):
+                if (dy, far) != (0, 0):
+                    send(2, at, precv.at[me], p_sem.at[0], rows_at[dy] + cols_at[far])
+
+    arrived(p_sem.at[0], some(precv, N - 1))
+    for h in range(2):
+        total = tree([precv[j, h].astype(F32) for j in range(N)])
+        column = block(rows_at[0] + quad + h * (NZ // 2))
+        midbuf[mine, h] = (hidden[:, column].astype(F32) + total).astype(BF16)
+    for (dy, dz), d in zip(MID_OFFSETS, MID_DISTANCE):
+        send(3, midbuf.at[mine], midbuf.at[mine], m_sem.at[mid_class(d)], rows_at[dy] + cols_at[dz])
+    sent(2, some(precv, N - 1))
 
     squares = jnp.zeros((seqs, 128), F32)
     gate = jnp.zeros((seqs, wg.shape[1]), F32)
     upper = jnp.zeros((seqs, wg.shape[1]), F32)
     for i, (least, most) in enumerate(MID_CLASSES):
-        near = at_distance(least, most)
+        near = [(-dy % NY, -dz % NZ) for (dy, dz), d in zip(MID_OFFSETS, MID_DISTANCE) if least <= d <= most]
         arrived(m_sem.at[i], some(midbuf, len(near)))
         if i == 0:
-            near = near + [me]
-        parts = []
-        for peer in near:
-            part = midbuf[peer].astype(F32)
-            squares = squares + part * part
-            parts.append((part * mgain_wide[pl.ds(peer, 1), :]).astype(BF16))
+            near = near + [(0, 0)]
+        parts, columns = [], []
+        for dy, dz in near:
+            low_z = jnp.bitwise_and(z + dz, NZ // 2 - 1)
+            pair = lax.shift_right_logical(rows_at[dy], 1) + low_z
+            for h in range(2):
+                column = rows_at[dy] + low_z + h * (NZ // 2)
+                part = midbuf[pair, h].astype(F32)
+                squares = squares + part * part
+                parts.append((part * mgain_wide[pl.ds(column, 1), :]).astype(BF16))
+                columns.append(column)
         left = jnp.concatenate(parts, axis=1)
-        gate = gate + dot_rows(left, jnp.concatenate([wg[p] for p in near], axis=1))
-        upper = upper + dot_rows(left, jnp.concatenate([wu[p] for p in near], axis=1))
+        gate = gate + jnp.dot(left, jnp.concatenate([wgt[p] for p in columns], axis=0), preferred_element_type=F32)
+        upper = upper + jnp.dot(left, jnp.concatenate([wut[p] for p in columns], axis=0), preferred_element_type=F32)
     scale = lax.rsqrt(row_sum(squares) / width + 1e-5)
     gate = gate * scale
     act = (gate / (1.0 + jnp.exp(-gate)) * (upper * scale)).astype(BF16)
     scatter(4, act, wd, dsend, drecv, d_sem)
-    sent(3, some(midbuf, N - 1))
+    sent(3, some(midbuf, len(MID_OFFSETS)))
     total = gathered(dsend, drecv, d_sem)
+    mid_own = midbuf[mine, lax.shift_right_logical(z, 2)]
     out_ref[...] = (mid_own.astype(F32) + total).astype(BF16)
     sent(4, some(dsend, N - 1))
 
@@ -367,18 +401,21 @@
             pltpu.VMEM((GROUP, 2, seqs, 128), BF16),
             pltpu.VMEM((N, 2, seqs, 128), BF16),
             pltpu.VMEM((N, 2, seqs, 128), BF16),
-            pltpu.VMEM(block, BF16),
-            pltpu.VMEM(block, BF16),
-            pltpu.VMEM(block, BF16),
+            pltpu.VMEM((N // 2, 2, seqs, 128), BF16),
+            pltpu.VMEM((N, 2, seqs, 128), BF16),
+            pltpu.VMEM((N // 2, 2, seqs, 128), BF16),
             pltpu.VMEM(block, BF16),
             pltpu.VMEM(block, BF16),
             pltpu.VMEM((lines, 128), F32),
+            pltpu.VMEM((KV_HEADS, seqs, HEAD_DIM, key_cache.shape[1]), BF16),
+            pltpu.VMEM((lines, 128, w_gate.shape[0]), BF16),
+            pltpu.VMEM((lines, 128, w_up.shape[0]), BF16),
             pltpu.SemaphoreType.DMA((len(operands),)),
             pltpu.SemaphoreType.DMA((6,)),
-            pltpu.SemaphoreType.DMA((KV_HEADS,)),
             pltpu.SemaphoreType.DMA((1,)),
-            pltpu.SemaphoreType.DMA((KV_HEADS,)),
+            pltpu.SemaphoreType.DMA((1,)),
             pltpu.SemaphoreType.DMA((2,)),
+            pltpu.SemaphoreType.DMA((1,)),
             pltpu.SemaphoreType.DMA((len(MID_CLASSES),)),
             pltpu.SemaphoreType.DMA((2,)),
         ],

time: 44.3 us -> 41.4 us (0.935)
  Pallas kernels: 43 us -> 40.1 us
    pallas_call x1, Pallas kernels: 43 us -> 40.1 us  [per_device(): pl.pallas_call(kernel, out_shape=jax.ShapeDtypeStruct((seqs, 128), BF16),...]
where the time goes in v4:
time: 41.4 us; the launch traced here: 41.3 us
  Pallas kernels  40.1 us (97%)
  local copies, waits for them, and re-layouts  1.26 us (3%)
    pallas_call x1, Pallas kernels, per_device(): pl.pallas_call(kernel, out_shape=jax.ShapeDtypeStruct((seqs, 128), BF16),...  40.1 us
    unnamed x1, local copies, waits for them, and re-layouts  1.26 us

profile of v4, /device:TPU:6, one launch (start us, length us, event | category | flops | bytes accessed | tf_op | source)
XLA Modules:
  0.0 41.3 jit_solution(2960431506561607064)
XLA Ops:
  0.0 40.1 %shard_map.136 = bf16[8,128]{1,0:T(8,128)(2,1)} custom-call(bf16[8,4096]{1,0:T(8,128)(2,1)} %hidden_hbm.1, bf16[32,128]{1,0:T(8,128)(2,1)} %bitcast.10, bf16[4096,128]{1,0:T(8,128)(2,1)} %wq_hbm.1, bf16[32,4096]{1,0:T(8,128)(2,1)} %bitcast.8, bf16[32,4096]{1,0:T(8,128)(2,1)} %bitcast.9, bf16[8,128,1024]{2,1,0:T(8,128)(2,1)} %kc_hbm.1, ...), custom_call_target="tpu_custom_call" | custom-call | tf_op jit(solution)/shard_map/pallas_call | solution.py:393
  40.1 1.3 %copy.16 = bf16[8,128]{1,0:T(8,128)(2,1)} copy(bf16[8,128]{1,0:T(8,128)(2,1)} %shard_map.136) | data formatting | bytes 4096

commit v5 on v4

--- a/solution.py
+++ b/solution.py
@@ -34,7 +34,7 @@
     key=lambda t: -(min(t[0], NY - t[0]) + min(t[1], NZ - t[1])),
 )
 MID_DISTANCE = [min(dy, NY - dy) + min(dz, NZ - dz) for dy, dz in MID_OFFSETS]
-MID_CLASSES = ((1, 2), (3, 3), (4, 4))
+MID_CLASSES = ((1, 1), (2, 2), (3, 3), (4, 4))
 
 
 def mid_class(distance):
@@ -259,8 +259,7 @@
     mgain_wide[...] = mgain[...].astype(F32)
 
     def level_of(stat):
-        pair = stat + pltpu.roll(stat, 1, 1)
-        return pair + pltpu.roll(pair, 2, 1)
+        return (stat + pltpu.roll(stat, 1, 1)) + (pltpu.roll(stat, 2, 1) + pltpu.roll(stat, 3, 1))
 
     def merge(state, parts):
         peak, weight_sum, number = state
@@ -392,7 +391,7 @@
     block = (N, seqs, 128)
     return pl.pallas_call(
         kernel,
-        out_shape=jax.ShapeDtypeStruct((seqs, 128), BF16),
+        out_shape=pltpu.VMEM((seqs, 128), BF16),
         in_specs=[pl.BlockSpec(memory_space=pltpu.HBM)] * len(operands),
         out_specs=pl.BlockSpec(memory_space=pltpu.VMEM),
         scratch_shapes=held
@@ -420,7 +419,7 @@
             pltpu.SemaphoreType.DMA((2,)),
         ],
         compiler_params=pltpu.CompilerParams(
-            collective_id=0, has_side_effects=True, vmem_limit_bytes=67043328
+            collective_id=0, has_side_effects=True, vmem_limit_bytes=67026944
         ),
     )(*operands)
 

time: 41.4 us -> 39.6 us (0.957)
  Pallas kernels: 40.1 us -> 39 us
  local copies, waits for them, and re-layouts: 1.26 us -> 0.58 us
    pallas_call x1, Pallas kernels: 40.1 us -> 39 us  [per_device(): pl.pallas_call(kernel, out_shape=pltpu.VMEM((seqs, 128), BF16), in_specs=...]
    unnamed x1, local copies, waits for them, and re-layouts: 1.26 us -> 0.58 us
where the time goes in v5:
time: 39.6 us
  Pallas kernels  39 us (98%)
  local copies, waits for them, and re-layouts  0.58 us (1%)
    pallas_call x1, Pallas kernels, per_device(): pl.pallas_call(kernel, out_shape=pltpu.VMEM((seqs, 128), BF16), in_specs=...  39 us

profile of v5, /device:TPU:6, one launch (start us, length us, event | category | flops | bytes accessed | tf_op | source)
XLA Modules:
  0.0 39.6 jit_solution(16715383972457452131)
XLA Ops:
  0.0 39.0 %shard_map.136 = bf16[8,128]{1,0:T(8,128)(2,1)S(1)} custom-call(bf16[8,4096]{1,0:T(8,128)(2,1)} %hidden_hbm.1, bf16[32,128]{1,0:T(8,128)(2,1)} %bitcast.10, bf16[4096,128]{1,0:T(8,128)(2,1)} %wq_hbm.1, bf16[32,4096]{1,0:T(8,128)(2,1)} %bitcast.8, bf16[32,4096]{1,0:T(8,128)(2,1)} %bitcast.9, bf16[8,128,1024]{2,1,0:T(8,128)(2,1)} %kc_hbm.1, ...), custom_call_target="tpu_custom_call" | custom-call | tf_op jit(solution)/shard_map/pallas_call | solution.py:392
  39.0 0.6 %copy.16 = bf16[8,128]{1,0:T(8,128)(2,1)} copy(bf16[8,128]{1,0:T(8,128)(2,1)S(1)} %shard_map.136) | data formatting | bytes 4096
